TPU v7x, 32 devices: a whole 2x2x4 slice. The times are simulated.
32 devices in a mesh: seq: 8 (over z, y), batch: 4 (over x, core).
Axes of the slice: x: 2, y: 2, z: 4, core: 2. Of those that a mesh axis runs over, the one named last changes fastest.
Arguments:
- conv_input: bfloat16 [4096, 8192], P(('batch', 'seq')), parts along dimension 0, may hold values from -6 to 6
- gate_input: bfloat16 [4096, 8192], P(('batch', 'seq')), parts along dimension 0, may hold values from -6 to 6
- conv_weight: bfloat16 [4, 8192], P(None, 'seq'), may hold values from -3 to 3
- conv_bias: bfloat16 [8192], P('seq'), may hold values from -3 to 3
- x_weight: bfloat16 [8192, 288], P('seq'), may hold values from -0.0625 to 0.0625
- dt_gain: float32 [256], replicated, may hold values from 0.5 to 1.5
- dt_weight: bfloat16 [256, 8192], P(None, 'seq'), may hold values from -0.375 to 0.375
- dt_bias: float32 [8192], P('seq'), may hold values from -6.9 to -2.3
- a_log: float32 [16, 8192], P(None, 'seq'), may hold values from 0 to 2.77
- skip: float32 [8192], P('seq'), may hold values from 0.5 to 1.5
Outputs:
- mixed: bfloat16 [4096, 8192], P(('batch', 'seq')), parts along dimension 0
There are 4 independent parts, one for each index of `batch`. A program takes and returns all parts, laid end to end along the dimension named above; an argument that names none is the same for every part. Nothing has to cross between parts.
All inputs are finite; a program needn't handle non-finite values.
Results may differ from a plain program's by a relative error of at most 0.0085.
Values may be sent and summed in bfloat16 or wider, within the bound.
A program may use at most 128 MiB of HBM per device.

v0:
```python
import functools

import jax
import jax.numpy as jnp
from jax import lax
from jax.experimental import pallas as pl
from jax.experimental.pallas import tpu as pltpu
from jax.sharding import Mesh
from jax.sharding import PartitionSpec as P

LOG2E = 1.4426950408889634
HALO = 8


MESH = pl.DeviceIdType.MESH


def pack(wide, exact):
    high = exact.astype(jnp.bfloat16)
    low = (exact - high.astype(jnp.float32)).astype(jnp.bfloat16)
    rest = -(2 * exact.shape[1]) % 128
    pieces = [wide.astype(jnp.bfloat16), high, low]
    if rest:
        pieces.append(jnp.zeros((exact.shape[0], rest), jnp.bfloat16))
    return jnp.concatenate(pieces, 1)


def place():
    x, y, core = lax.axis_index("x"), lax.axis_index("y"), lax.axis_index("core")
    return (core * lax.axis_size("x") + x) * lax.axis_size("y") + y


def device(index):
    ys, xs = lax.axis_size("y"), lax.axis_size("x")
    part = index // ys
    return {"x": lax.rem(part, xs), "y": lax.rem(index, ys), "core": part // xs}


def greet(peers):
    me = place()
    barrier = pltpu.get_barrier_semaphore()
    for k in range(1, peers):
        pl.semaphore_signal(
            barrier, inc=1, device_id=device(lax.rem(me + k, peers)), device_id_type=MESH
        )
    pl.semaphore_wait(barrier, peers - 1)
    return me


def reduce_kernel(peers, rank, states2, part_ref, gain_ref, out_ref, got, send_sem, recv_sem):
    rows = got.shape[1]
    me = greet(peers)
    spread = []
    for k in range(1, peers):
        other = lax.rem(me + k, peers)
        copy = pltpu.make_async_remote_copy(
            src_ref=part_ref.at[pl.ds(pl.multiple_of(other * rows, rows), rows)],
            dst_ref=got.at[k],
            send_sem=send_sem.at[0, k],
            recv_sem=recv_sem.at[0, k],
            device_id=device(other),
            device_id_type=MESH,
        )
        copy.start()
        spread.append(copy)
    mine = pl.ds(pl.multiple_of(me * rows, rows), rows)
    total = part_ref[mine, :].astype(jnp.float32)
    for k in range(1, peers):
        spread[k - 1].wait_recv()
        total = total + got[k].astype(jnp.float32)
    low = total[:, :rank]
    exact = total[:, rank : rank + states2] + total[:, rank + states2 : rank + 2 * states2]
    normed = low * lax.rsqrt(jnp.mean(low * low, axis=1, keepdims=True) + 1e-06) * gain_ref[...]
    out_ref[mine, :] = pack(normed, exact)
    gather = []
    for k in range(1, peers):
        copy = pltpu.make_async_remote_copy(
            src_ref=out_ref.at[mine],
            dst_ref=out_ref.at[mine],
            send_sem=send_sem.at[1, k],
            recv_sem=recv_sem.at[1, k],
            device_id=device(lax.rem(me + k, peers)),
            device_id_type=MESH,
        )
        copy.start()
        gather.append(copy)
    for k in range(1, peers):
        spread[k - 1].wait_send()
        gather[k - 1].wait()


def reduce_norm(partial, gain, peers, rank, states2):
    total, cols = partial.shape
    return pl.pallas_call(
        functools.partial(reduce_kernel, peers, rank, states2),
        in_specs=[pl.BlockSpec(memory_space=pltpu.VMEM)] * 2,
        out_specs=pl.BlockSpec(memory_space=pltpu.VMEM),
        out_shape=jax.ShapeDtypeStruct((total, cols), jnp.bfloat16),
        scratch_shapes=[
            pltpu.VMEM((peers, total // peers, cols), jnp.bfloat16),
            pltpu.SemaphoreType.DMA((2, peers)),
            pltpu.SemaphoreType.DMA((2, peers)),
        ],
        compiler_params=pltpu.CompilerParams(collective_id=0, has_side_effects=True),
        name="reduce_norm",
    )(partial, gain[None, :])


def conv_kernel(width, rank, x_ref, halo_ref, w_ref, b_ref, xw_ref, xc_ref, part_ref, prev):
    rows, chans = x_ref.shape
    chunk = min(chans, 256)

    @pl.when(pl.program_id(1) == 0)
    def _():
        prev[...] = halo_ref[0]

    for start in range(0, chans, chunk):
        sl = slice(start, start + chunk)
        cur = x_ref[:, sl].astype(jnp.float32)
        ext = jnp.concatenate([prev[:, sl], cur], 0)
        total = b_ref[:, sl] + jnp.zeros((rows, chunk), jnp.float32)
        for tap in range(width):
            low = HALO - width + 1 + tap
            total = total + w_ref[tap : tap + 1, sl] * ext[low : low + rows]
        xc_ref[:, sl] = (total / (1.0 + jnp.exp(-total))).astype(jnp.bfloat16)
        prev[:, sl] = cur[rows - HALO :]
    part = jnp.dot(xc_ref[...], xw_ref[...], preferred_element_type=jnp.float32)
    part_ref[...] = pack(part[:, :rank], part[:, rank:])


def conv_project(arrived, halo, weight, bias, x_weight, parts, block, rank):
    total, chans = arrived.shape
    steps = total // parts // block
    cols = x_weight.shape[1]
    width = weight.shape[0]
    packed = rank + -(-2 * (cols - rank) // 128) * 128
    whole = lambda p, i: (0, 0)
    return pl.pallas_call(
        functools.partial(conv_kernel, width, rank),
        grid=(parts, steps),
        in_specs=[
            pl.BlockSpec((block, chans), lambda p, i: (p * steps + i, 0)),
            pl.BlockSpec((1, HALO, chans), lambda p, i: (p, 0, 0)),
            pl.BlockSpec((width, chans), whole),
            pl.BlockSpec((1, chans), whole),
            pl.BlockSpec((chans, cols), whole),
        ],
        out_specs=[
            pl.BlockSpec((block, chans), lambda p, i: (p * steps + i, 0)),
            pl.BlockSpec((block, packed), lambda p, i: (p * steps + i, 0)),
        ],
        out_shape=[
            jax.ShapeDtypeStruct((total, chans), jnp.bfloat16),
            jax.ShapeDtypeStruct((total, packed), jnp.bfloat16),
        ],
        scratch_shapes=[pltpu.VMEM((HALO, chans), jnp.float32)],
        name="conv_project",
    )(arrived, halo, weight.astype(jnp.float32), bias.astype(jnp.float32)[None, :], x_weight)


def prepare_kernel(
    states, xc_ref, nm_ref, bc_ref, dtw_ref, dtb_ref, rate_ref, st, dr, end_ref, sum_ref
):
    rows, chans = xc_ref.shape
    group = chans // 128

    @pl.when(pl.program_id(1) == 0)
    def _():
        end_ref[...] = jnp.zeros_like(end_ref)
        sum_ref[...] = jnp.zeros_like(sum_ref)

    raw = jnp.dot(nm_ref[...], dtw_ref[...], preferred_element_type=jnp.float32) + dtb_ref[...]
    step = jnp.maximum(raw, 0.0) + jnp.log1p(jnp.exp(-jnp.abs(raw)))
    drive = step * xc_ref[...].astype(jnp.float32)
    for j in range(group):
        st[pl.ds(j, rows, stride=group), :] = step[:, j * 128 : (j + 1) * 128]
        dr[pl.ds(j, rows, stride=group), :] = drive[:, j * 128 : (j + 1) * 128]

    rates = [rate_ref[n * group : (n + 1) * group, :] for n in range(states)]

    def advance(t, carry):
        at = pl.ds(pl.multiple_of(t * group, group), group)
        s = st[at, :]
        d = dr[at, :]
        base = t * (2 * states)
        after = [
            jnp.exp2(s * rates[n]) * carry[n] + bc_ref[0, 0, base + n] * d for n in range(states)
        ]
        return tuple(after) + (carry[states] + s,)

    carry = tuple(end_ref[0, n * group : (n + 1) * group, :] for n in range(states))
    carry = lax.fori_loop(0, rows, advance, carry + (sum_ref[0],), unroll=4)
    for n in range(states):
        end_ref[0, n * group : (n + 1) * group, :] = carry[n]
    sum_ref[0] = carry[states]


def prepare(xc, normed, bc, dt_weight, dt_bias, rate2, first, parts, steps, block):
    chans = xc.shape[1]
    states2 = bc.shape[2] // block
    states = states2 // 2
    group = chans // 128
    rank = normed.shape[1]
    whole = lambda p, i: (0, 0)
    tile = lambda p, i: ((first + p) * steps + i, 0)
    mine = lambda p, i: (p * steps + i, 0)
    total = parts * steps * block
    return pl.pallas_call(
        functools.partial(prepare_kernel, states),
        grid=(parts, steps),
        in_specs=[
            pl.BlockSpec((block, chans), tile),
            pl.BlockSpec((block, rank), tile),
            pl.BlockSpec(
                (1, 1, block * states2),
                lambda p, i: ((first + p) * steps + i, 0, 0),
                memory_space=pltpu.SMEM,
            ),
            pl.BlockSpec((rank, chans), whole),
            pl.BlockSpec((1, chans), whole),
            pl.BlockSpec((states * group, 128), whole),
        ],
        out_specs=[
            pl.BlockSpec((block * group, 128), mine),
            pl.BlockSpec((block * group, 128), mine),
            pl.BlockSpec((1, states * group, 128), lambda p, i: (p, 0, 0)),
            pl.BlockSpec((1, group, 128), lambda p, i: (p, 0, 0)),
        ],
        out_shape=[
            jax.ShapeDtypeStruct((total * group, 128), jnp.float32),
            jax.ShapeDtypeStruct((total * group, 128), jnp.float32),
            jax.ShapeDtypeStruct((parts, states * group, 128), jnp.float32),
            jax.ShapeDtypeStruct((parts, group, 128), jnp.float32),
        ],
        cost_estimate=pl.CostEstimate(
            flops=total * chans * (2 * rank + 5 * states),
            bytes_accessed=total * chans * 10,
            transcendentals=total * chans * states,
        ),
        name="prepare",
    )(xc, normed, bc, dt_weight, dt_bias, rate2)


def scan_kernel(
    states, parts, peers, xc_ref, st, dr, bc_ref, rate_ref, skip_ref, h0_ref, out_ref,
    ybuf, ys, hs, send_sem, recv_sem, own_sem,
):
    total, chans = xc_ref.shape
    group = chans // 128
    rows = total // peers
    steps = total // parts // rows
    xs = lax.axis_size("x")
    cores = parts // xs
    x = lax.axis_index("x")
    me = greet(peers)
    columns = out_ref.at[:, pl.ds(pl.multiple_of(me * chans, chans), chans)]
    rates = [rate_ref[n * group : (n + 1) * group, :] for n in range(states)]

    def send(block):
        away = lax.rem(block - me + peers, peers)
        return pltpu.make_async_remote_copy(
            src_ref=ybuf.at[block],
            dst_ref=columns,
            send_sem=send_sem.at[away],
            recv_sem=recv_sem.at[away],
            device_id=device(block),
            device_id_type=MESH,
        )

    own = pltpu.make_async_copy(ybuf.at[me], columns, own_sem)

    def one_block(place_in_order, _):
        turn, i = place_in_order // steps, lax.rem(place_in_order, steps)
        part = lax.rem(turn, cores) * xs + lax.rem(x + 1 + turn // cores, xs)
        block = part * steps + i
        base_row = pl.multiple_of(block * rows, rows)

        @pl.when(i == 0)
        def _():
            hs[...] = h0_ref[part].astype(jnp.float32)

        def advance(t, hidden):
            at = pl.ds(pl.multiple_of((base_row + t) * group, group), group)
            s = st[at, :]
            d = dr[at, :]
            base = (base_row + t) * (2 * states)
            after = []
            sums = [None, None]
            for n in range(states):
                h = jnp.exp2(s * rates[n]) * hidden[n] + bc_ref[base + n] * d
                after.append(h)
                term = bc_ref[base + states + n] * h
                sums[n % 2] = term if sums[n % 2] is None else sums[n % 2] + term
            ys[pl.ds(pl.multiple_of(t * group, group), group), :] = sums[0] + sums[1]
            return tuple(after)

        hidden = tuple(hs[n * group : (n + 1) * group, :] for n in range(states))
        hidden = lax.fori_loop(0, rows, advance, hidden, unroll=4)
        for n in range(states):
            hs[n * group : (n + 1) * group, :] = hidden[n]
        for j in range(group):
            sl = slice(j * 128, (j + 1) * 128)
            skipped = skip_ref[:, sl] * xc_ref[pl.ds(base_row, rows), sl].astype(jnp.float32)
            y = ys[pl.ds(j, rows, stride=group), :] + skipped
            ybuf[block, :, sl] = y.astype(jnp.bfloat16)

        @pl.when(block == me)
        def _():
            own.start()

        @pl.when(block != me)
        def _():
            send(block).start()

        return 0

    lax.fori_loop(0, peers, one_block, 0)
    own.wait()
    for k in range(1, peers):
        send(lax.rem(me + k, peers)).wait()


def scan(xc, st, dr, bc, rate2, skip, start, parts, peers):
    total, chans = xc.shape
    states = bc.shape[0] // total // 2
    group = chans // 128
    rows = total // peers
    vmem = pl.BlockSpec(memory_space=pltpu.VMEM)
    return pl.pallas_call(
        functools.partial(scan_kernel, states, parts, peers),
        in_specs=[vmem, vmem, vmem, pl.BlockSpec(memory_space=pltpu.SMEM), vmem, vmem, vmem],
        out_specs=pl.BlockSpec(memory_space=pl.ANY),
        out_shape=jax.ShapeDtypeStruct((rows, peers * chans), jnp.bfloat16),
        scratch_shapes=[
            pltpu.VMEM((peers, rows, chans), jnp.bfloat16),
            pltpu.VMEM((rows * group, 128), jnp.float32),
            pltpu.VMEM((states * group, 128), jnp.float32),
            pltpu.SemaphoreType.DMA((peers,)),
            pltpu.SemaphoreType.DMA((peers,)),
            pltpu.SemaphoreType.DMA,
        ],
        compiler_params=pltpu.CompilerParams(collective_id=1, has_side_effects=True),
        name="selective_scan",
    )(xc, st, dr, bc, rate2, skip, start)


PLANE = ("core", "x", "y")


def local(
    sizes,
    conv_input,
    gate_input,
    conv_weight,
    conv_bias,
    x_weight,
    dt_gain,
    dt_weight,
    dt_bias,
    a_log,
    skip,
):
    depth, parts = sizes
    rank, chans = dt_weight.shape
    states = a_log.shape[0]
    rows = conv_input.shape[0]
    group = chans // 128
    cores = parts // lax.axis_size("x")
    place = lambda z, b: z * parts + b % (parts // cores) * cores + b // (parts // cores)
    swap = [(place(a, b), place(b, a)) for a in range(depth) for b in range(parts)]
    move = lambda v: lax.ppermute(v, ("z", "x", "core"), swap)
    following = [(z, z + 1) for z in range(depth - 1)]
    onward = lambda v: lax.ppermute(v, "z", following)

    conv_pack = move(jnp.concatenate([conv_weight, conv_bias[None, :]], 0))
    x_weight = move(x_weight)
    dt_weight = move(dt_weight)
    scan_pack = move(jnp.concatenate([a_log, dt_bias[None, :], skip[None, :]], 0))
    width = conv_weight.shape[0]
    conv_weight, conv_bias = conv_pack[:width], conv_pack[width]

    arrived = lax.all_to_all(conv_input, PLANE, split_axis=1, concat_axis=0, tiled=True)
    span = arrived.shape[0] // parts
    halo = onward(arrived.reshape(parts, span, chans)[:, span - HALO :]).astype(jnp.float32)
    conv_out, partial_value = conv_project(
        arrived, halo, conv_weight, conv_bias, x_weight, parts, rows, rank
    )
    everyone = reduce_norm(partial_value, dt_gain, arrived.shape[0] // rows, rank, 2 * states)
    normed_all = everyone[:, :rank]
    bc_all = everyone[:, rank : rank + 2 * states].astype(jnp.float32) + everyone[
        :, rank + 2 * states : rank + 4 * states
    ].astype(jnp.float32)
    bc_all = bc_all.reshape(-1, 1, rows * 2 * states)
    rate2 = (-jnp.exp(scan_pack[:states]) * LOG2E).reshape(states * group, 128)
    dt_bias, skip = scan_pack[states : states + 1], scan_pack[states + 1 :]
    steps = span // rows
    st, dr, ends, sums = prepare(
        conv_out, normed_all, bc_all, dt_weight, dt_bias, rate2, 0, parts, steps, rows
    )
    decay = jnp.exp2(sums[:, None] * rate2.reshape(1, states, group, 128)).reshape(ends.shape)
    start = onward(ends.astype(jnp.bfloat16))
    for _ in range(depth - 2):
        start = onward((decay * start.astype(jnp.float32) + ends).astype(jnp.bfloat16))
    returned = scan(
        conv_out, st, dr, bc_all.reshape(-1), rate2, skip, start, parts, arrived.shape[0] // rows
    )
    return (returned.astype(jnp.float32) * jax.nn.silu(gate_input.astype(jnp.float32))).astype(
        jnp.bfloat16
    )


def solution(mesh):
    seq, batch = mesh.shape["seq"], mesh.shape["batch"]
    cores = 2
    grid = Mesh(
        mesh.devices.reshape(batch, seq // batch, batch // cores, cores), ("z", "y", "x", "core")
    )
    seqs = ("z", "y")
    rows = P(("x", "core", "z", "y"), None)
    return jax.shard_map(
        functools.partial(local, (batch, batch)),
        mesh=grid,
        in_specs=(
            rows,
            rows,
            P(None, seqs),
            P(seqs),
            P(seqs, None),
            P(),
            P(None, seqs),
            P(seqs),
            P(None, seqs),
            P(seqs),
        ),
        out_specs=rows,
        check_vma=False,
    )
```

profile of v0, /device:TPU:21, one launch (start us, length us, event | category | flops | bytes accessed | tf_op | source)
XLA Modules:
  0.0 196.7 jit_solution(6166070009690305414)
XLA Ops:
  0.0 3.2 %copy.21 = bf16[16,8,8,1024]{3,2,0,1:T(8,128)(2,1)} copy(bf16[16,8,8,1024]{3,2,1,0:T(8,128)(2,1)} %bitcast.33) | data formatting | bytes 4194304 | tf_op jit(solution)/shard_map/all_to_all | solution.py:382
  3.3 4.5 %all-to-all-start = ((bf16[128,8,1024]{2,0,1:T(8,128)(2,1)}), bf16[128,8,1024]{2,0,1:T(8,128)(2,1)S(1)}, u32[]{:S(2)}, u32[]{:S(2)}) async-start(bf16[128,8,1024]{2,0,1:T(8,128)(2,1)} %bitcast.32), calls=%async_computation | async-start | bytes 4194304 | tf_op jit(solution)/shard_map/all_to_all | solution.py:382
  9.2 1.5 collective-permute-start.3
  10.7 1.7 collective-permute-start.2
  13.6 43.2 %all-to-all-done = bf16[128,8,1024]{2,0,1:T(8,128)(2,1)S(1)} async-done(((bf16[128,8,1024]{2,0,1:T(8,128)(2,1)}), bf16[128,8,1024]{2,0,1:T(8,128)(2,1)S(1)}, u32[]{:S(2)}, u32[]{:S(2)}) %all-to-all-start) | async-done | bytes 2097184 | tf_op jit(solution)/shard_map/all_to_all | solution.py:382
  56.8 1.9 collective-permute-start
  60.0 1.2 copy.17.xw_ref
  62.5 8.6 %conv_project.1 = (bf16[1024,1024]{1,0:T(8,128)(2,1)}, bf16[1024,384]{1,0:T(8,128)(2,1)}) custom-call(bf16[1024,1024]{1,0:T(8,128)(2,1)} %bitcast.31, f32[4,8,1024]{2,1,0:T(8,128)} %convert_element_type.40.halo_ref, f32[4,1024]{1,0:T(4,128)} %slice_convert_fusion.w_ref, f32[1,1024]{1,0:T(1,128)} %slice_convert_fusion.1.b_ref, bf16[1024,288]{1,0:T(8,128)(2,1)} %copy.17.xw_ref), custom_call_target="tpu_custom_call" | custom-call | tf_op jit(solution)/shard_map/conv_project/pallas_call | solution.py:138
  71.1 28.1 %reduce_norm.1 = bf16[1024,384]{1,0:T(8,128)(2,1)} custom-call(bf16[1024,384]{1,0:T(8,128)(2,1)} %get-tuple-element.12.part_ref, f32[1,256]{1,0:T(1,128)} %bitcast.36), custom_call_target="tpu_custom_call" | custom-call | tf_op jit(solution)/shard_map/reduce_norm/pallas_call | solution.py:94
  99.3 1.9 slice.30.nm_ref
  101.1 1.2 convert_add_fusion
  102.3 0.9 reshape.22.bc_ref
  103.3 22.0 %prepare.1 = (f32[8192,128]{1,0:T(8,128)}, f32[8192,128]{1,0:T(8,128)}, f32[4,128,128]{2,1,0:T(8,128)}, f32[4,8,128]{2,1,0:T(8,128)}) custom-call(bf16[1024,1024]{1,0:T(8,128)(2,1)} %get-tuple-element.11.xc_ref, bf16[1024,256]{1,0:T(8,128)(2,1)} %slice.30.nm_ref, f32[8,1,4096]{2,1,0:T(1,128)} %reshape.22.bc_ref, ...), custom_call_target="tpu_custom_call" | custom-call | flops 620756992 | bytes 10485760 | tf_op jit(solution)/shard_map/prepare/pallas_call | solution.py:208
  125.2 1.0 convert_element_type.45
  126.2 3.2 %collective-permute-start.5 = (bf16[4,128,128]{2,1,0:T(8,128)(2,1)S(1)}, bf16[4,128,128]{2,1,0:T(8,128)(2,1)S(1)}, u32[]{:S(2)}, u32[]{:S(2)}) collective-permute-start(bf16[4,128,128]{2,1,0:T(8,128)(2,1)S(1)} %convert_element_type.45), channel_id=1, source_target_pairs={{0,8},{8,16},{16,24},{1,9},{9,17},{17,25},{2,10},{10,18},{18,26},{... | collective-permute-start | bytes 393224 | tf_op jit(solution)/shard_map/ppermute | solution.py:373
  129.4 3.3 %collective-permute-done.5 = bf16[4,128,128]{2,1,0:T(8,128)(2,1)S(1)} collective-permute-done((bf16[4,128,128]{2,1,0:T(8,128)(2,1)S(1)}, bf16[4,128,128]{2,1,0:T(8,128)(2,1)S(1)}, u32[]{:S(2)}, u32[]{:S(2)}) %collective-permute-start.5) | collective-permute-done | bytes 131104 | tf_op jit(solution)/shard_map/ppermute | solution.py:373
  132.7 1.0 fusion.10
  133.7 2.4 %collective-permute-start.6 = (bf16[4,128,128]{2,1,0:T(8,128)(2,1)S(1)}, bf16[4,128,128]{2,1,0:T(8,128)(2,1)S(1)}, u32[]{:S(2)}, u32[]{:S(2)}) collective-permute-start(bf16[4,128,128]{2,1,0:T(8,128)(2,1)S(1)} %fusion.10), channel_id=1, source_target_pairs={{0,8},{8,16},{16,24},{1,9},{9,17},{17,25},{2,10},{10,18},{18,26},{... | collective-permute-start | bytes 393224 | tf_op jit(solution)/shard_map/ppermute | solution.py:373
  136.1 3.3 %collective-permute-done.6 = bf16[4,128,128]{2,1,0:T(8,128)(2,1)S(1)} collective-permute-done((bf16[4,128,128]{2,1,0:T(8,128)(2,1)S(1)}, bf16[4,128,128]{2,1,0:T(8,128)(2,1)S(1)}, u32[]{:S(2)}, u32[]{:S(2)}) %collective-permute-start.6) | collective-permute-done | bytes 131104 | tf_op jit(solution)/shard_map/ppermute | solution.py:373
  139.4 1.0 fusion.12
  140.5 2.4 %collective-permute-start.7 = (bf16[4,128,128]{2,1,0:T(8,128)(2,1)S(1)}, bf16[4,128,128]{2,1,0:T(8,128)(2,1)S(1)}, u32[]{:S(2)}, u32[]{:S(2)}) collective-permute-start(bf16[4,128,128]{2,1,0:T(8,128)(2,1)S(1)} %fusion.12), channel_id=1, source_target_pairs={{0,8},{8,16},{16,24},{1,9},{9,17},{17,25},{2,10},{10,18},{18,26},{... | collective-permute-start | bytes 393224 | tf_op jit(solution)/shard_map/ppermute | solution.py:373
  143.7 2.5 %collective-permute-done.7.h0_ref = bf16[4,128,128]{2,1,0:T(8,128)(2,1)S(1)} collective-permute-done((bf16[4,128,128]{2,1,0:T(8,128)(2,1)S(1)}, bf16[4,128,128]{2,1,0:T(8,128)(2,1)S(1)}, u32[]{:S(2)}, u32[]{:S(2)}) %collective-permute-start.7) | collective-permute-done | bytes 131104 | tf_op jit(solution)/shard_map/ppermute | solution.py:373
  146.8 45.7 %selective_scan.1 = bf16[128,8192]{1,0:T(8,128)(2,1)} custom-call(bf16[1024,1024]{1,0:T(8,128)(2,1)} %get-tuple-element.11.xc_ref, f32[8192,128]{1,0:T(8,128)} %get-tuple-element.13.st, f32[8192,128]{1,0:T(8,128)} %get-tuple-element.14.dr, f32[32768]{0:T(1024)} %reshape_reshape.4.bc_ref, f32[128,128]{1,0:T(8,128)} %reshape.21.rate_ref, ...), custom_call_target="tpu_custom_call" | custom-call | tf_op jit(solution)/shard_map/selective_scan/pallas_call | solution.py:329
  192.5 4.2 %fusion.4 = bf16[128,8192]{1,0:T(8,128)(2,1)} fusion(bf16[128,8192]{1,0:T(8,128)(2,1)S(1)} %copy-done.1, bf16[128,8192]{1,0:T(8,128)(2,1)} %selective_scan.1), kind=kLoop, calls=%fused_computation.6 | loop fusion | flops 8388608 | bytes 6291456 | tf_op jit(solution)/shard_map/convert_element_type | solution.py:407
  (38 shorter events, 6.7 us)
Async XLA Ops:
  0.0 7.8 %copy-start.8 = (bf16[1024]{0:T(1024)(128)(2,1)S(1)}, bf16[1024]{0:T(1024)(128)(2,1)}, u32[]{:S(2)}) copy-start(bf16[1024]{0:T(1024)(128)(2,1)} %param.13) | copy-start | bytes 6148
  0.0 7.8 %copy-start.5 = (bf16[4,1024]{1,0:T(4,128)(2,1)S(1)}, bf16[4,1024]{1,0:T(4,128)(2,1)}, u32[]{:S(2)}) copy-start(bf16[4,1024]{1,0:T(4,128)(2,1)} %param.12) | copy-start | bytes 24580
  0.0 8.5 %copy-start.4 = (f32[16,1024]{1,0:T(8,128)S(1)}, f32[16,1024]{1,0:T(8,128)}, u32[]{:S(2)}) copy-start(f32[16,1024]{1,0:T(8,128)} %param.18) | copy-start | bytes 196612
  0.0 8.5 %copy-start.6 = (f32[1024]{0:T(1024)S(1)}, f32[1024]{0:T(1024)}, u32[]{:S(2)}) copy-start(f32[1024]{0:T(1024)} %param.19) | copy-start | bytes 12292
  0.0 8.5 %copy-start.7 = (f32[1024]{0:T(1024)S(1)}, f32[1024]{0:T(1024)}, u32[]{:S(2)}) copy-start(f32[1024]{0:T(1024)} %param.17) | copy-start | bytes 12292
  0.0 9.2 %copy-start.9 = (bf16[256,1024]{1,0:T(8,128)(2,1)S(1)}, bf16[256,1024]{1,0:T(8,128)(2,1)}, u32[]{:S(2)}) copy-start(bf16[256,1024]{1,0:T(8,128)(2,1)} %param.16) | copy-start | bytes 1572868
  3.3 53.6 %all-to-all-start = ((bf16[128,8,1024]{2,0,1:T(8,128)(2,1)}), bf16[128,8,1024]{2,0,1:T(8,128)(2,1)S(1)}, u32[]{:S(2)}, u32[]{:S(2)}) async-start(bf16[128,8,1024]{2,0,1:T(8,128)(2,1)} %bitcast.32), calls=%async_computation | async-start | bytes 4194304 | tf_op jit(solution)/shard_map/all_to_all | solution.py:382
  7.8 4.6 %collective-permute-start.1 = (bf16[5,1024]{1,0:T(8,128)(2,1)S(1)}, bf16[5,1024]{1,0:T(8,128)(2,1)S(1)}, u32[]{:S(2)}, u32[]{:S(2)}) collective-permute-start(bf16[5,1024]{1,0:T(8,128)(2,1)S(1)} %pad_maximum_fusion.1), channel_id=1, source_target_pairs={{0,0},{2,8},{1,16},{3,24},{8,2},{10,10},{9,18},{11,26},{16,1},{18,... | collective-permute-start | bytes 30728 | tf_op jit(solution)/shard_map/ppermute | solution.py:371
  8.5 5.1 %collective-permute-start.4 = (f32[18,1024]{1,0:T(8,128)S(1)}, f32[18,1024]{1,0:T(8,128)S(1)}, u32[]{:S(2)}, u32[]{:S(2)}) collective-permute-start(f32[18,1024]{1,0:T(8,128)S(1)} %pad_maximum_fusion), channel_id=1, source_target_pairs={{0,0},{2,8},{1,16},{3,24},{8,2},{10,10},{9,18},{11,26},{16,1},{18,... | collective-permute-start | bytes 221192 | tf_op jit(solution)/shard_map/ppermute | solution.py:371
  9.2 94.0 %collective-permute-start.3 = (bf16[256,1024]{1,0:T(8,128)(2,1)S(1)}, bf16[256,1024]{1,0:T(8,128)(2,1)}, u32[]{:S(2)}, u32[]{:S(2)}) collective-permute-start(bf16[256,1024]{1,0:T(8,128)(2,1)S(1)} %copy-done.9), channel_id=1, source_target_pairs={{0,0},{2,8},{1,16},{3,24},{8,2},{10,10},{9,18},{11,26},{16,1},{18,... | collective-permute-start | bytes 1572872 | tf_op jit(solution)/shard_map/ppermute | solution.py:371
  10.7 49.3 %collective-permute-start.2 = (bf16[1024,288]{0,1:T(8,128)(2,1)}, bf16[1024,288]{0,1:T(8,128)(2,1)S(1)}, u32[]{:S(2)}, u32[]{:S(2)}) collective-permute-start(bf16[1024,288]{0,1:T(8,128)(2,1)} %param.14), channel_id=1, source_target_pairs={{0,0},{2,8},{1,16},{3,24},{8,2},{10,10},{9,18},{11,26},{16,1},{18,... | collective-permute-start | bytes 1769480 | tf_op jit(solution)/shard_map/ppermute | solution.py:371
  56.8 5.7 %copy-start = (bf16[128,8,1024]{2,0,1:T(8,128)(2,1)}, bf16[128,8,1024]{2,0,1:T(8,128)(2,1)S(1)}, u32[]{:S(2)}) copy-start(bf16[128,8,1024]{2,0,1:T(8,128)(2,1)S(1)} %all-to-all-done) | copy-start | bytes 6291460
  56.8 5.0 %collective-permute-start = (bf16[4,8,1024]{2,1,0:T(8,128)(2,1)S(1)}, bf16[4,8,1024]{2,1,0:T(8,128)(2,1)S(1)}, u32[]{:S(2)}, u32[]{:S(2)}) collective-permute-start(bf16[4,8,1024]{2,1,0:T(8,128)(2,1)S(1)} %slice.36), channel_id=1, source_target_pairs={{0,8},{8,16},{16,24},{1,9},{9,17},{17,25},{2,10},{10,18},{18,26},{... | collective-permute-start | bytes 196616 | tf_op jit(solution)/shard_map/ppermute | solution.py:373
  103.3 29.4 %copy-start.2 = (f32[128,128]{1,0:T(8,128)S(1)}, f32[128,128]{1,0:T(8,128)}, u32[]{:S(2)}) copy-start(f32[128,128]{1,0:T(8,128)} %reshape.21.rate_ref) | copy-start | bytes 196612
  126.2 6.5 %collective-permute-start.5 = (bf16[4,128,128]{2,1,0:T(8,128)(2,1)S(1)}, bf16[4,128,128]{2,1,0:T(8,128)(2,1)S(1)}, u32[]{:S(2)}, u32[]{:S(2)}) collective-permute-start(bf16[4,128,128]{2,1,0:T(8,128)(2,1)S(1)} %convert_element_type.45), channel_id=1, source_target_pairs={{0,8},{8,16},{16,24},{1,9},{9,17},{17,25},{2,10},{10,18},{18,26},{... | collective-permute-start | bytes 393224 | tf_op jit(solution)/shard_map/ppermute | solution.py:373
  133.7 5.7 %collective-permute-start.6 = (bf16[4,128,128]{2,1,0:T(8,128)(2,1)S(1)}, bf16[4,128,128]{2,1,0:T(8,128)(2,1)S(1)}, u32[]{:S(2)}, u32[]{:S(2)}) collective-permute-start(bf16[4,128,128]{2,1,0:T(8,128)(2,1)S(1)} %fusion.10), channel_id=1, source_target_pairs={{0,8},{8,16},{16,24},{1,9},{9,17},{17,25},{2,10},{10,18},{18,26},{... | collective-permute-start | bytes 393224 | tf_op jit(solution)/shard_map/ppermute | solution.py:373
  140.5 5.7 %collective-permute-start.7 = (bf16[4,128,128]{2,1,0:T(8,128)(2,1)S(1)}, bf16[4,128,128]{2,1,0:T(8,128)(2,1)S(1)}, u32[]{:S(2)}, u32[]{:S(2)}) collective-permute-start(bf16[4,128,128]{2,1,0:T(8,128)(2,1)S(1)} %fusion.12), channel_id=1, source_target_pairs={{0,8},{8,16},{16,24},{1,9},{9,17},{17,25},{2,10},{10,18},{18,26},{... | collective-permute-start | bytes 393224 | tf_op jit(solution)/shard_map/ppermute | solution.py:373
  146.2 0.7 copy-start.3
  146.8 45.7 %copy-start.1 = (bf16[128,8192]{1,0:T(8,128)(2,1)S(1)}, bf16[128,8192]{1,0:T(8,128)(2,1)}, u32[]{:S(2)}) copy-start(bf16[128,8192]{1,0:T(8,128)(2,1)} %param.11) | copy-start | bytes 6291460
where the time goes:
time: 197 us
  Pallas kernels  104 us (53%)
  waiting for transfers between devices  52.9 us (27%)
  starting transfers between devices  18.9 us (10%)
  other arithmetic  10.4 us (5%)
  local copies, waits for them, and re-layouts  9.97 us (5%)
    pallas_call x1, Pallas kernels, scan(): pl.pallas_call(functools.partial(scan_kernel, states, parts, peers), in_s...  45.7 us
    all_to_all x1, waiting for transfers between devices, local(): lax.all_to_all(conv_input, PLANE, split_axis=1, concat_axis=0, tiled=True)  43.2 us
    pallas_call x1, Pallas kernels, reduce_norm(): pl.pallas_call(functools.partial(reduce_kernel, peers, rank, states2), in...  28.1 us
    pallas_call x1, Pallas kernels, prepare(): pl.pallas_call(functools.partial(prepare_kernel, states), grid=(parts, st...  22 us
    ppermute x4, starting transfers between devices, local(): onward = lambda v: lax.ppermute(v, 'z', following)  9.93 us
    ppermute x4, waiting for transfers between devices, local(): onward = lambda v: lax.ppermute(v, 'z', following)  9.66 us
    pallas_call x1, Pallas kernels, conv_project(): pl.pallas_call(functools.partial(conv_kernel, width, rank), grid=(parts,...  8.63 us
    all_to_all x1, starting transfers between devices, local(): lax.all_to_all(conv_input, PLANE, split_axis=1, concat_axis=0, tiled=True)  4.51 us
  transfers between devices with their start and end apart: 9, of which 5 were waited for; matrix products, arithmetic and copies ran while one was open for 5% of the time, Pallas kernels for 19%

commit v1 on v0

v1 whole, which is shorter than its diff:
```python
import functools
import math

import jax
import jax.numpy as jnp
from jax import lax
from jax.experimental import pallas as pl
from jax.experimental.pallas import tpu as pltpu
from jax.sharding import Mesh
from jax.sharding import PartitionSpec as P

LOG2E = 1.4426950408889634
LN2 = 0.6931471805599453
LANES = 128
ROWS8 = 8
PACK = 16
WIDE = 256
GROUP = 1024
MESH = pl.DeviceIdType.MESH
F32 = jnp.float32
BF16 = jnp.bfloat16


def split_rows(rows, planes):
    half = rows // 2
    if planes == 2:
        private = -(-half // (3 * PACK)) * PACK
        return half, private, half - 2 * private
    return half, half // planes, 0


def padded_rows(rows, planes):
    unit = 2 * PACK * (planes if planes > 2 else 1)
    return -(-rows // unit) * unit


class Gather:
    def __init__(self, sizes, place, which, buf, sems):
        self.A, self.B, self.X = sizes
        self.a, self.b, self.x, self.c = place
        self.w = which
        self.buf = buf
        (self.zs, self.ys, self.xs, self.ds, self.wr, self.xr, self.dr) = sems
        self.half, self.private, self.shared = split_rows(buf.shape[1], self.X)

    def shard(self, i):
        A, B = self.A, self.B
        return lax.rem(self.a - lax.rem(i, A) + A, A) * B + lax.rem(self.b - i // A + B, B)

    def window(self, s, core):
        start = core * self.half + self.x * self.private
        return self.buf.at[s, pl.ds(pl.multiple_of(start, PACK), self.private + self.shared)]

    def own(self, s, core, plane):
        start = core * self.half + plane * (self.private + self.shared)
        return self.buf.at[s, pl.ds(pl.multiple_of(start, PACK), self.private)]

    def copy(self, ref, send, recv, **to):
        return pltpu.make_async_remote_copy(
            src_ref=ref, dst_ref=ref, send_sem=send, recv_sem=recv,
            device_id=to, device_id_type=MESH,
        )

    def along(self, j):
        return self.copy(
            self.window(self.a * self.B + self.b, self.c), self.zs.at[self.w, j], self.wr.at[self.w, j],
            a=lax.rem(self.a + j, self.A),
        )

    def across(self, i, k):
        return self.copy(
            self.window(self.shard(i), self.c), self.ys.at[self.w, k, i],
            self.wr.at[self.w, k * self.A + i], b=lax.rem(self.b + k, self.B),
        )

    def plane(self, i, k):
        return self.copy(
            self.own(self.shard(i), self.c, self.x), self.xs.at[self.w, k, i],
            self.xr.at[self.w, k, i], x=lax.rem(self.x + k, self.X),
        )

    def from_plane(self, i, k):
        ref = self.own(self.shard(i), self.c, lax.rem(self.x - k + self.X, self.X))
        return self.copy(ref, self.xs.at[self.w, k, i], self.xr.at[self.w, k, i], x=self.x)

    def pair(self, i, e, core):
        s = self.shard(i)
        if e == 0:
            ref = self.window(s, core)
        else:
            ref = self.own(s, core, lax.rem(self.x - e + self.X, self.X))
        return self.copy(ref, self.ds.at[self.w, e, i], self.dr.at[self.w, e, i], c=1 - self.c)

    def begin(self):
        for j in range(1, self.A):
            self.along(j).start()
        for k in range(1, self.B):
            self.across(0, k).start()

    def relay(self, i):
        pltpu.make_async_remote_copy(
            src_ref=self.window(self.shard(i), self.c), dst_ref=self.window(self.shard(i), self.c),
            send_sem=self.zs.at[self.w, 0], recv_sem=self.wr.at[self.w, i],
            device_id={"c": self.c}, device_id_type=MESH,
        ).wait_recv()

        @pl.when(i < self.A)
        def _():
            for k in range(1, self.B):
                self.across(i, k).start()

        for k in range(1, self.X):
            self.plane(i, k).start()
        self.pair(i, 0, self.c).start()

    def relay_plane(self, i):
        for k in range(1, self.X):
            self.from_plane(i, k).wait_recv()
            self.pair(i, k, self.c).start()

    def ready(self, i):
        for e in range(self.X):
            self.pair(i, e, 1 - self.c).wait_recv()

    def drain(self):
        for j in range(1, self.A):
            self.along(j).wait_send()
        for k in range(1, self.B):
            lax.fori_loop(0, self.A, lambda i, _: (self.across(i, k).wait_send(), 0)[1], 0)

        def one(i, _):
            for k in range(1, self.X):
                self.plane(i, k).wait_send()
            for e in range(self.X):
                self.pair(i, e, self.c).wait_send()
            return 0

        lax.fori_loop(1, self.A * self.B, one, 0)


def scan_tokens(st, dr, bx, rate, hidden, tokens, unroll, each=None):
    tiles = GROUP // LANES
    rates = [[rate[8 * k : 8 * k + 8, LANES * j : LANES * j + LANES] for j in range(tiles)] for k in range(2)]

    def body(i, carry):
        h = [list(carry[:tiles]), list(carry[tiles:])]
        for u in range(unroll):
            at = pl.multiple_of((i * unroll + u) * 16, 16)
            b = [bx[pl.ds(at + 8 * k, 8), :] for k in range(2)]
            block = i * (unroll // ROWS8) + u // ROWS8
            row = slice(u % ROWS8, u % ROWS8 + 1)
            for j in range(tiles):
                cols = slice(LANES * j, LANES * j + LANES)
                s = jnp.broadcast_to(st[block, row, cols], (ROWS8, LANES))
                d = jnp.broadcast_to(dr[block, row, cols], (ROWS8, LANES))
                for k in range(2):
                    h[k][j] = jnp.exp2(s * rates[k][j]) * h[k][j] + b[k] * d
                if each is not None:
                    each(i, u, j, h[0][j], h[1][j])
        if each is not None:
            each(i, None, None, None, None)
        return tuple(h[0]) + tuple(h[1])

    return lax.fori_loop(0, tokens // unroll, body, hidden)


def mixer_kernel(
    sizes, states,
    x_hbm, g_hbm, xw_hbm, dtw_hbm, pk_hbm, gain_ref,
    out_hbm,
    xv, gv, xwv, dtv, pkv, halo, cp, w1, w2, acc, acc2, nm, bx, cblk, st, dr, rt, hs,
    eb, rb, sb, h0b,
    lsem, osem, hsem, csem_s, csem_r,
    zs, ys, xs, ds, wr, xr, dr_sem,
    es, er, bs, br,
):
    A, B, X = sizes
    D = A * B
    tokens, inner = xv.shape
    shard = pkv.shape[1]
    nb = shard // WIDE
    rank = gain_ref.shape[1]
    extra = 2 * states
    groups = inner // GROUP
    span = rank + 3 * PACK
    a, b, x, c = (lax.axis_index(n) for n in ("a", "b", "x", "c"))
    me = a * B + b
    place = (a, b, x, c)
    sems = (zs, ys, xs, ds, wr, xr, dr_sem)

    loads = [
        pltpu.make_async_copy(src, dst, lsem.at[n])
        for n, (src, dst) in enumerate(((pk_hbm, pkv), (xw_hbm, xwv), (dtw_hbm, dtv), (x_hbm, xv), (g_hbm, gv)))
    ]
    for load in loads:
        load.start()

    barrier = pltpu.get_barrier_semaphore()
    for r in range(1, D):
        other = lax.rem(me + r, D)
        pl.semaphore_signal(
            barrier, inc=1, device_id={"a": other // B, "b": lax.rem(other, B)}, device_id_type=MESH
        )
    for k in range(1, X):
        pl.semaphore_signal(barrier, inc=1, device_id={"x": lax.rem(x + k, X)}, device_id_type=MESH)
    pl.semaphore_signal(barrier, inc=1, device_id={"c": 1 - c}, device_id_type=MESH)

    loads[0].wait()
    for j in range(nb):
        cols = slice(WIDE * j, WIDE * j + WIDE)
        cp[me, j] = pkv[0:ROWS8, cols]
        rate = -jnp.exp(pkv[ROWS8 : ROWS8 + states, cols]) * LOG2E
        high = rate.astype(BF16)
        base = j * span + rank
        w2[me, base : base + states, :] = high
        w2[me, base + PACK : base + PACK + states, :] = (rate - high.astype(F32)).astype(BF16)
        two = pkv[5:7, cols]
        top = two.astype(BF16).astype(F32)
        w2[me, base + 2 * PACK : base + 3 * PACK, :] = jnp.concatenate(
            [top, two - top, jnp.zeros((PACK - 4, WIDE), F32)], 0
        ).astype(BF16)
    loads[1].wait()
    w1[me, 0:shard, :] = xwv[:, 0:rank]
    pick = (
        lax.broadcasted_iota(jnp.int32, (extra, rank + extra), 1)
        == lax.broadcasted_iota(jnp.int32, (extra, rank + extra), 0) + rank
    ).astype(BF16)
    for j in range(nb):
        turned = lax.dot_general(
            pick, xwv[WIDE * j : WIDE * j + WIDE, :], (((1,), (1,)), ((), ())), preferred_element_type=F32
        )
        w1[me, shard + extra * j : shard + extra * j + extra, :] = turned.astype(BF16)
    pl.semaphore_wait(barrier, D - 1 + X - 1 + 1)

    def pack_copy(r):
        other = lax.rem(me + r, D)
        return pltpu.make_async_remote_copy(
            src_ref=cp.at[me], dst_ref=cp.at[me], send_sem=csem_s.at[r], recv_sem=csem_r.at[r],
            device_id={"a": other // B, "b": lax.rem(other, B)}, device_id_type=MESH,
        )

    after = lax.rem(me + 1, D)
    halo_copy = pltpu.make_async_remote_copy(
        src_ref=x_hbm.at[pl.ds(tokens - ROWS8, ROWS8)], dst_ref=halo, send_sem=hsem.at[0], recv_sem=hsem.at[1],
        device_id={"a": after // B, "b": lax.rem(after, B)}, device_id_type=MESH,
    )
    for r in range(1, D):
        pack_copy(r).start()
    halo_copy.start()

    first = Gather(sizes, place, 0, w1, sems)
    second = Gather(sizes, place, 1, w2, sems)
    first.begin()

    loads[2].wait()
    for j in range(nb):
        w2[me, j * span : j * span + rank, :] = dtv[:, WIDE * j : WIDE * j + WIDE]

    for r in range(1, D):
        other = lax.rem(me - r + D, D)
        pltpu.make_async_remote_copy(
            src_ref=cp.at[other], dst_ref=cp.at[other], send_sem=csem_s.at[r], recv_sem=csem_r.at[r],
            device_id={"c": c}, device_id_type=MESH,
        ).wait_recv()
    halo_copy.wait_recv()
    loads[3].wait()
    lead = (me > 0).astype(F32)

    def convolve(q, _):
        cols = pl.ds(pl.multiple_of(q * WIDE, WIDE), WIDE)
        taps = cp.at[q // nb, lax.rem(q, nb)]
        cur = xv[:, cols].astype(F32)
        ext = jnp.concatenate([halo[:, cols].astype(F32) * lead, cur], 0)
        total = taps[4:5, :] + taps[3:4, :] * cur
        for tap in range(3):
            low = ROWS8 - 3 + tap
            total = total + taps[tap : tap + 1, :] * ext[low : low + tokens]
        xv[:, cols] = (total / (1.0 + jnp.exp(-total))).astype(BF16)
        return 0

    lax.fori_loop(0, inner // WIDE, convolve, 0)

    def relay_first(i, _):
        first.relay(i)

        @pl.when(i > 1)
        def _():
            first.relay_plane(i - 1)

        return 0

    lax.fori_loop(1, A, relay_first, 0)
    second.begin()
    lax.fori_loop(A, D, relay_first, 0)
    first.relay_plane(D - 1)

    acc[...] = jnp.zeros_like(acc)
    acc2[...] = jnp.zeros_like(acc2)

    def project(i, _):
        @pl.when(i > 0)
        def _():
            first.ready(i)

        s = first.shard(i)
        base = pl.multiple_of(s * shard, WIDE)
        acc[...] += jnp.dot(xv[:, pl.ds(base, shard)], w1[s, 0:shard, :], preferred_element_type=F32)
        for j in range(nb):
            acc2[...] += lax.dot_general(
                xv[:, pl.ds(base + WIDE * j, WIDE)], w1[s, shard + extra * j : shard + extra * j + extra, :],
                (((1,), (1,)), ((), ())), preferred_element_type=F32,
            )
        return 0

    lax.fori_loop(0, D, project, 0)

    low = acc[...]
    nm[...] = (
        low * lax.rsqrt(jnp.mean(low * low, axis=1, keepdims=True) + 1e-06) * gain_ref[...]
    ).astype(BF16)
    bc = acc2[...]
    for n in range(states):
        bx[pl.ds(n, tokens, stride=states), :] = jnp.broadcast_to(bc[:, n : n + 1], (tokens, LANES))
    lane = lax.broadcasted_iota(jnp.int32, (extra, PACK * states), 1)
    spread = (
        lax.broadcasted_iota(jnp.int32, (extra, PACK * states), 0) == states + lax.rem(lane, states)
    ).astype(BF16)
    tiled = jnp.dot(bc.astype(BF16), spread, preferred_element_type=F32)
    slot = lax.broadcasted_iota(jnp.int32, tiled.shape, 1) // states
    turn = lax.rem(lax.broadcasted_iota(jnp.int32, tiled.shape, 0), PACK)
    cblk[...] = jnp.where(slot == turn, tiled, 0.0).astype(BF16)

    tiles = GROUP // LANES
    blocks = GROUP // WIDE
    local_order = groups == D

    def group_at(i):
        return second.shard(i) if local_order else i

    def to_combiner(g):
        return pltpu.make_async_remote_copy(
            src_ref=eb.at[g], dst_ref=rb.at[me], send_sem=es.at[g], recv_sem=er.at[me],
            device_id={"a": g // B, "b": lax.rem(g, B)}, device_id_type=MESH,
        )

    def pass_one(i, _):
        if local_order:
            @pl.when(i + 2 < D)
            def _():
                second.relay(i + 2)

            @pl.when(i + 1 < D)
            def _():
                second.relay_plane(i + 1)

            @pl.when(i > 0)
            def _():
                second.ready(i)

        g = group_at(i)
        sums = []
        for q in range(blocks):
            cb = g * blocks + q
            s, j = cb // nb, lax.rem(cb, nb)
            cols = pl.ds(pl.multiple_of(cb * WIDE, WIDE), WIDE)
            base = pl.multiple_of(j * span, PACK)
            rows = lambda n: pl.ds(pl.multiple_of(base + rank + n * PACK, PACK), PACK)
            misc = w2[s, rows(2), :].astype(F32)
            rt[g, :, WIDE * q : WIDE * q + WIDE] = w2[s, rows(0), :].astype(F32) + w2[s, rows(1), :].astype(F32)
            raw = jnp.dot(nm[...], w2[s, pl.ds(base, rank), :], preferred_element_type=F32)
            raw = raw + (misc[0:1] + misc[2:3])
            small = jnp.exp2(jnp.abs(raw) * -LOG2E)
            step = jnp.maximum(raw, 0.0) + LN2 * jnp.log2(1.0 + small)
            st[:, :, cols] = step.reshape(tokens // ROWS8, ROWS8, WIDE)
            dr[:, :, cols] = (step * xv[:, cols].astype(F32)).reshape(tokens // ROWS8, ROWS8, WIDE)
            total = jnp.sum(step, axis=0, keepdims=True)
            sums += [total[:, :LANES], total[:, LANES:]]
        view = pl.ds(pl.multiple_of(g * GROUP, GROUP), GROUP)
        zero = jnp.zeros((ROWS8, LANES), F32)
        h = scan_tokens(
            st.at[:, :, view], dr.at[:, :, view], bx, rt.at[g], (zero,) * (2 * tiles), tokens, ROWS8
        )
        for j in range(tiles):
            eb[g, 16 * j : 16 * j + 16, :] = jnp.concatenate([h[j], h[tiles + j]], 0).astype(BF16)
        sums = jnp.concatenate(sums, 0)
        top = sums.astype(BF16).astype(F32)
        eb[g, 16 * tiles : 16 * tiles + 16, :] = jnp.concatenate([top, sums - top], 0).astype(BF16)

        @pl.when(g != me)
        def _():
            to_combiner(g).start()

        @pl.when(g == me)
        def _():
            rb[me] = eb[me]

        return 0

    if local_order:
        second.relay(1)
    else:
        def settle(i, _):
            second.relay(i)
            second.relay_plane(i)
            second.ready(i)
            return 0

        lax.fori_loop(1, D, settle, 0)
    lax.fori_loop(0, groups, pass_one, 0)

    def to_owner(k):
        return pltpu.make_async_remote_copy(
            src_ref=sb.at[k], dst_ref=h0b.at[me], send_sem=bs.at[k], recv_sem=br.at[me],
            device_id={"a": k // B, "b": lax.rem(k, B)}, device_id_type=MESH,
        )

    def arrival(k):
        return pltpu.make_async_remote_copy(
            src_ref=rb.at[k], dst_ref=rb.at[k], send_sem=es.at[0], recv_sem=er.at[k],
            device_id={"c": c}, device_id_type=MESH,
        )

    @pl.when(me < groups)
    def _():
        def combine(k, start):
            @pl.when(k != me)
            def _():
                arrival(k).wait_recv()

            now = []
            both = rb[k, 16 * tiles : 16 * tiles + 16, :].astype(F32)
            sums = both[0:8] + both[8:16]
            for j in range(tiles):
                sb[k, 16 * j : 16 * j + 16, :] = start[j].astype(BF16)
                decay = jnp.exp2(sums[j : j + 1, :] * rt[me, :, LANES * j : LANES * j + LANES])
                now.append(decay * start[j] + rb[k, 16 * j : 16 * j + 16, :].astype(F32))

            @pl.when(k != me)
            def _():
                to_owner(k).start()

            @pl.when(k == me)
            def _():
                h0b[me] = sb[me]

            return tuple(now)

        lax.fori_loop(0, D, combine, (jnp.zeros((16, LANES), F32),) * tiles)

    loads[4].wait()

    def start_of(g):
        return pltpu.make_async_remote_copy(
            src_ref=h0b.at[g], dst_ref=h0b.at[g], send_sem=bs.at[0], recv_sem=br.at[g],
            device_id={"c": c}, device_id_type=MESH,
        )

    def put(g):
        view = pl.ds(pl.multiple_of(g * GROUP, GROUP), GROUP)
        return pltpu.make_async_copy(gv.at[:, view], out_hbm.at[:, view], osem.at[g])

    def pass_two(g, _):
        @pl.when(g != me)
        def _():
            start_of(g).wait_recv()

        first_state = [h0b[g, 16 * j : 16 * j + 16, :].astype(F32) for j in range(tiles)]
        h = tuple(v[:8] for v in first_state) + tuple(v[8:] for v in first_state)
        view = pl.ds(pl.multiple_of(g * GROUP, GROUP), GROUP)
        xg, gg = xv.at[:, view], gv.at[:, view]
        direct = []
        for q in range(blocks):
            cb = g * blocks + q
            s, j = cb // nb, lax.rem(cb, nb)
            misc = w2[s, pl.ds(pl.multiple_of(j * span + rank + 2 * PACK, PACK), PACK), :].astype(F32)
            direct.append(misc[1:2] + misc[3:4])

        def each(i, u, j, lo, hi):
            if u is not None:
                hs[16 * u : 16 * u + 16, LANES * j : LANES * j + LANES] = jnp.concatenate([lo, hi], 0).astype(BF16)
                return
            rows = pl.ds(pl.multiple_of(i * PACK, PACK), PACK)
            for q in range(blocks):
                cols = slice(WIDE * q, WIDE * q + WIDE)
                y = jnp.dot(cblk[rows, :], hs[:, cols], preferred_element_type=F32)
                y = y + direct[q] * xg[rows, cols].astype(F32)
                gate = gg[rows, cols].astype(F32)
                gg[rows, cols] = (y * gate / (1.0 + jnp.exp(-gate))).astype(BF16)

        scan_tokens(st.at[:, :, view], dr.at[:, :, view], bx, rt.at[g], h, tokens, PACK, each)
        put(g).start()
        return 0

    lax.fori_loop(0, groups, pass_two, 0)

    def finish(g, _):
        put(g).wait()

        @pl.when(g != me)
        def _():
            to_combiner(g).wait_send()

        return 0

    lax.fori_loop(0, groups, finish, 0)

    @pl.when(me < groups)
    def _():
        def sent(k, _):
            @pl.when(k != me)
            def _():
                to_owner(k).wait_send()

            return 0

        lax.fori_loop(0, D, sent, 0)

    for r in range(1, D):
        pack_copy(r).wait_send()
    halo_copy.wait_send()
    first.drain()
    second.drain()


def local(sizes, conv_input, gate_input, conv_weight, conv_bias, x_weight, dt_gain, dt_weight, dt_bias, a_log, skip):
    A, B, X = sizes
    D = A * B
    tokens, inner = conv_input.shape
    rank, shard = dt_weight.shape
    states = a_log.shape[0]
    extra = x_weight.shape[1] - rank
    nb = shard // WIDE
    groups = inner // GROUP
    pack = jnp.concatenate(
        [conv_weight.astype(F32), conv_bias.astype(F32)[None], dt_bias[None], skip[None],
         jnp.zeros((1, shard), F32), a_log], 0
    )
    r1 = padded_rows(shard + extra * nb, X)
    r2 = padded_rows((rank + 3 * PACK) * nb, X)
    tiles = GROUP // LANES
    packet = 16 * tiles + 16
    hbm = pl.BlockSpec(memory_space=pl.ANY)
    vmem = pl.BlockSpec(memory_space=pltpu.VMEM)
    dma = pltpu.SemaphoreType.DMA
    return pl.pallas_call(
        functools.partial(mixer_kernel, sizes, states),
        in_specs=[hbm] * 5 + [vmem],
        out_specs=hbm,
        out_shape=jax.ShapeDtypeStruct((tokens, inner), BF16),
        scratch_shapes=[
            pltpu.VMEM((tokens, inner), BF16),
            pltpu.VMEM((tokens, inner), BF16),
            pltpu.VMEM(x_weight.shape, BF16),
            pltpu.VMEM(dt_weight.shape, BF16),
            pltpu.VMEM(pack.shape, F32),
            pltpu.VMEM((ROWS8, inner), BF16),
            pltpu.VMEM((D, nb, ROWS8, WIDE), F32),
            pltpu.VMEM((D, r1, WIDE), BF16),
            pltpu.VMEM((D, r2, WIDE), BF16),
            pltpu.VMEM((tokens, rank), F32),
            pltpu.VMEM((tokens, extra), F32),
            pltpu.VMEM((tokens, rank), BF16),
            pltpu.VMEM((tokens * states, LANES), F32),
            pltpu.VMEM((tokens, PACK * states), BF16),
            pltpu.VMEM((tokens // ROWS8, ROWS8, inner), F32),
            pltpu.VMEM((tokens // ROWS8, ROWS8, inner), F32),
            pltpu.VMEM((groups, states, GROUP), F32),
            pltpu.VMEM((PACK * states, GROUP), BF16),
            pltpu.VMEM((groups, packet, LANES), BF16),
            pltpu.VMEM((D, packet, LANES), BF16),
            pltpu.VMEM((D, 16 * tiles, LANES), BF16),
            pltpu.VMEM((groups, 16 * tiles, LANES), BF16),
            dma((5,)), dma((groups,)), dma((2,)), dma((D,)), dma((D,)),
            dma((2, A)), dma((2, B, A)), dma((2, X, D)), dma((2, X, D)),
            dma((2, D)), dma((2, X, D)), dma((2, X, D)),
            dma((groups,)), dma((D,)), dma((D,)), dma((groups,)),
        ],
        compiler_params=pltpu.CompilerParams(
            collective_id=0, has_side_effects=True, vmem_limit_bytes=60 * 1024 * 1024
        ),
        name="mixer",
    )(conv_input, gate_input, x_weight, dt_weight, pack, dt_gain[None, :])


def solution(mesh):
    seq, batch = mesh.shape["seq"], mesh.shape["batch"]
    cores = 2
    A = math.gcd(seq, batch)
    B, X = seq // A, batch // cores
    grid = Mesh(mesh.devices.reshape(A, B, X, cores), ("a", "b", "x", "c"))
    seqs = ("a", "b")
    rows = P(("x", "c", "a", "b"), None)
    return jax.shard_map(
        functools.partial(local, (A, B, X)),
        mesh=grid,
        in_specs=(
            rows, rows, P(None, seqs), P(seqs), P(seqs, None), P(), P(None, seqs), P(seqs), P(None, seqs), P(seqs),
        ),
        out_specs=rows,
        check_vma=False,
    )
```

time: 197 us -> 123 us (0.62)
  the two profiles are of different devices: /device:TPU:21 before, /device:TPU:28 now
where the time goes in v1:
time: 123 us
  Pallas kernels  114 us (93%)
  local copies, waits for them, and re-layouts  8.13 us (7%)
    pallas_call x1, Pallas kernels, local(): pl.pallas_call(functools.partial(mixer_kernel, sizes, states), in_specs=[...  114 us
    unnamed x2, local copies, waits for them, and re-layouts  5.31 us
    concatenate x1, local copies, waits for them, and re-layouts, local(): jnp.concatenate([conv_weight.astype(F32), conv_bias.astype(F32)[None], dt...  2.82 us

profile of v1, /device:TPU:28, one launch (start us, length us, event | category | flops | bytes accessed | tf_op | source)
XLA Modules:
  0.0 122.5 jit_solution(3222597074271751319)
XLA Ops:
  0.0 0.7 broadcast_in_dim.24
  0.7 2.8 %concatenate.3.pk_hbm = f32[24,1024]{1,0:T(8,128)} concatenate(bf16[4,1024]{1,0:T(4,128)(2,1)} %param.12, f32[1,1024]{1,0:T(1,128)S(1)} %bitcast.4, f32[1,1024]{1,0:T(1,128)} %bitcast.5, f32[1,1024]{1,0:T(1,128)} %bitcast.6, f32[1,1024]{1,0:T(1,128)S(1)} %broadcast_in_dim.22, f32[16,1024]{1,0:T(8,128)} %param.18), dimensions={0} | concatenate | bytes 188416 | tf_op jit(solution)/shard_map/concatenate | solution.py:534
  3.5 2.2 %copy.11.xw_hbm = bf16[1024,288]{1,0:T(8,128)(2,1)} copy(bf16[1024,288]{0,1:T(8,128)(2,1)} %param.14) | data formatting | bytes 1179648 | tf_op args[4]
  5.7 113.7 %mixer.1 = bf16[128,8192]{1,0:T(8,128)(2,1)} custom-call(bf16[128,8192]{1,0:T(8,128)(2,1)} %x_hbm.1, bf16[128,8192]{1,0:T(8,128)(2,1)} %g_hbm.1, bf16[1024,288]{1,0:T(8,128)(2,1)} %copy.11.xw_hbm, bf16[256,1024]{1,0:T(8,128)(2,1)} %dtw_hbm.1, f32[24,1024]{1,0:T(8,128)} %concatenate.3.pk_hbm, f32[1,256]{1,0:T(1,128)} %bitcast.7), custom_call_target="tpu_custom_call" | custom-call | tf_op jit(solution)/shard_map/mixer/pallas_call | solution.py:545
  119.4 3.1 %copy.13 = bf16[128,8192]{1,0:T(8,128)(2,1)} copy(bf16[128,8192]{1,0:T(8,128)(2,1)} %mixer.1) | data formatting | bytes 4194304
  (1 shorter events, 0.0 us)

commit v2 on v1

v2 whole, which is shorter than its diff:
```python
import functools
import math

import jax
import jax.numpy as jnp
from jax import lax
from jax.experimental import pallas as pl
from jax.experimental.pallas import tpu as pltpu
from jax.sharding import Mesh
from jax.sharding import PartitionSpec as P

LOG2E = 1.4426950408889634
LN2 = 0.6931471805599453
LANES = 128
ROWS8 = 8
PACK = 16
WIDE = 256
GROUP = 1024
STEP = 16
TILES = 4
PITCH = 9
MESH = pl.DeviceIdType.MESH
F32 = jnp.float32
BF16 = jnp.bfloat16


def split_rows(rows, planes):
    half = rows // 2
    if planes == 2:
        private = -(-half // (3 * PACK)) * PACK
        return half, private, half - 2 * private
    return half, half // planes, 0


def padded_rows(rows, planes):
    unit = 2 * PACK * (planes if planes > 2 else 1)
    return -(-rows // unit) * unit


def column(a, i, size):
    turn = lax.rem(i, 2)
    inner = a + (1 - 2 * turn) * ((i + 1) // 2)
    outer = jnp.where(2 * a < size - 1, i, size - 1 - i)
    return jnp.where(i <= 2 * jnp.minimum(a, size - 1 - a), inner, outer)


class Gather:
    def __init__(self, sizes, place, which, buf, sems, small=None, small_sems=None):
        self.A, self.B, self.X = sizes
        self.a, self.b, self.x, self.c = place
        self.w = which
        self.buf = buf
        (self.zs, self.ys, self.xs, self.ds, self.wr, self.xr, self.dr) = sems
        self.small = small
        self.small_sems = small_sems
        self.half, self.private, self.shared = split_rows(buf.shape[1], self.X)

    def shard(self, i):
        a = column(self.a, lax.rem(i, self.A), self.A)
        return a * self.B + lax.rem(self.b - i // self.A + self.B, self.B)

    def window(self, s, core):
        start = core * self.half + self.x * self.private
        return self.buf.at[s, pl.ds(pl.multiple_of(start, PACK), self.private + self.shared)]

    def own(self, s, core, plane):
        start = core * self.half + plane * (self.private + self.shared)
        return self.buf.at[s, pl.ds(pl.multiple_of(start, PACK), self.private)]

    def copy(self, ref, send, recv, **to):
        return pltpu.make_async_remote_copy(
            src_ref=ref, dst_ref=ref, send_sem=send, recv_sem=recv,
            device_id=to, device_id_type=MESH,
        )

    def along(self, p, way):
        s = p * self.B + self.b
        to = self.a + 1 - 2 * way
        out = []
        if self.small is not None:
            zs, _, wr = self.small_sems
            out.append(self.copy(self.small.at[s], zs.at[way, p], wr.at[s], a=to))
        out.append(self.copy(self.window(s, self.c), self.zs.at[self.w, way, p], self.wr.at[self.w, s], a=to))
        return out

    def across(self, p, k):
        s = p * self.B + self.b
        to = lax.rem(self.b + k, self.B)
        out = []
        if self.small is not None:
            _, ys, wr = self.small_sems
            out.append(self.copy(self.small.at[s], ys.at[k, p], wr.at[s], b=to))
        out.append(self.copy(self.window(s, self.c), self.ys.at[self.w, k, p], self.wr.at[self.w, s], b=to))
        return out

    def plane(self, s, k):
        return self.copy(
            self.own(s, self.c, self.x), self.xs.at[self.w, k, s],
            self.xr.at[self.w, k, s], x=lax.rem(self.x + k, self.X),
        )

    def from_plane(self, s, k):
        ref = self.own(s, self.c, lax.rem(self.x - k + self.X, self.X))
        return self.copy(ref, self.xs.at[self.w, k, s], self.xr.at[self.w, k, s], x=self.x)

    def pair(self, s, e, core):
        if e == 0:
            ref = self.window(s, core)
        else:
            ref = self.own(s, core, lax.rem(self.x - e + self.X, self.X))
        return self.copy(ref, self.ds.at[self.w, e, s], self.dr.at[self.w, e, s], c=1 - self.c)

    def sends(self, p, right, left, run):
        @pl.when(right & (self.a + 1 < self.A))
        def _():
            run(self.along(p, 0))

        @pl.when(left & (self.a > 0))
        def _():
            run(self.along(p, 1))

    @staticmethod
    def start(copies):
        for copy in copies:
            copy.start()

    @staticmethod
    def sent(copies):
        for copy in copies:
            copy.wait_send()

    def begin(self):
        self.sends(self.a, self.a >= 0, self.a >= 0, self.start)
        for k in range(1, self.B):
            self.start(self.across(self.a, k))

    def relay(self, i):
        s = self.shard(i)
        p = s // self.B
        if self.small is not None:
            zs, _, wr = self.small_sems
            self.copy(self.small.at[s], zs.at[0, 0], wr.at[s], c=self.c).wait_recv()
        self.copy(self.window(s, self.c), self.zs.at[self.w, 0, 0], self.wr.at[self.w, s], c=self.c).wait_recv()

        @pl.when(i < self.A)
        def _():
            self.sends(p, p < self.a, p > self.a, self.start)
            for k in range(1, self.B):
                self.start(self.across(p, k))

        for k in range(1, self.X):
            self.plane(s, k).start()
        self.pair(s, 0, self.c).start()

    def relay_plane(self, i):
        s = self.shard(i)
        for k in range(1, self.X):
            self.from_plane(s, k).wait_recv()
            self.pair(s, k, self.c).start()

    def ready(self, i):
        s = self.shard(i)
        for e in range(self.X):
            self.pair(s, e, 1 - self.c).wait_recv()

    def drain(self):
        def line(p, _):
            self.sends(p, p <= self.a, p >= self.a, self.sent)
            for k in range(1, self.B):
                self.sent(self.across(p, k))
            return 0

        lax.fori_loop(0, self.A, line, 0)

        def one(i, _):
            s = self.shard(i)
            for k in range(1, self.X):
                self.plane(s, k).wait_send()
            for e in range(self.X):
                self.pair(s, e, self.c).wait_send()
            return 0

        lax.fori_loop(1, self.A * self.B, one, 0)


def scan_tokens(st, dr, bx, rate, hidden, tokens, tiles, each=None):
    rates = [[rate[8 * k : 8 * k + 8, cols] for cols in tiles] for k in range(2)]
    count = len(tiles)

    def body(i, carry):
        h = [list(carry[:count]), list(carry[count:])]
        for u in range(STEP):
            at = pl.multiple_of((i * STEP + u) * 16, 16)
            b = [bx[pl.ds(at + 8 * k, 8), :] for k in range(2)]
            block = i * (STEP // ROWS8) + u // ROWS8
            row = slice(u % ROWS8, u % ROWS8 + 1)
            for j, cols in enumerate(tiles):
                s = jnp.broadcast_to(st[block, row, cols], (ROWS8, LANES))
                d = jnp.broadcast_to(dr[block, row, cols], (ROWS8, LANES))
                for k in range(2):
                    h[k][j] = jnp.exp2(s * rates[k][j]) * h[k][j] + b[k] * d
            if each is not None:
                each(i, u, at, h)
        return tuple(h[0]) + tuple(h[1])

    return lax.fori_loop(0, tokens // STEP, body, hidden)


def silu(v):
    half = 0.5 * v
    return half + half * jnp.tanh(half)


def mixer_kernel(
    sizes, states,
    x_hbm, g_hbm, xw_hbm, dtw_hbm, cw_ref, cb_ref, db_ref, sk_ref, al_ref, gain_ref,
    out_hbm,
    xv, gv, xwv, dtv, halo, cp, w1, w2, acc, nm, bx, cx, st, dr, rt, zb,
    eb, rb, sb, h0b,
    lsem, osem, hsem, cz, cy, cr,
    zs, ys, xs, ds, wr, xr, dr_sem,
    es, er, bs, br,
):
    A, B, X = sizes
    D = A * B
    tokens, inner = xv.shape
    wide, shard = xwv.shape
    nb = shard // WIDE
    rank = gain_ref.shape[1]
    taps = cw_ref.shape[0]
    groups = inner // GROUP
    span = rank + 3 * PACK
    a, b, x, c = (lax.axis_index(n) for n in ("a", "b", "x", "c"))
    me = a * B + b
    place = (a, b, x, c)
    sems = (zs, ys, xs, ds, wr, xr, dr_sem)

    loads = [
        pltpu.make_async_copy(src, dst, lsem.at[n])
        for n, (src, dst) in enumerate(((xw_hbm, xwv), (dtw_hbm, dtv), (x_hbm, xv), (g_hbm, gv)))
    ]
    for load in loads:
        load.start()

    barrier = pltpu.get_barrier_semaphore()
    for r in range(1, D):
        other = lax.rem(me + r, D)
        pl.semaphore_signal(
            barrier, inc=1, device_id={"a": other // B, "b": lax.rem(other, B)}, device_id_type=MESH
        )
    for k in range(1, X):
        pl.semaphore_signal(barrier, inc=1, device_id={"x": lax.rem(x + k, X)}, device_id_type=MESH)
    pl.semaphore_signal(barrier, inc=1, device_id={"c": 1 - c}, device_id_type=MESH)

    rows = [cw_ref[...].astype(F32), cb_ref[...].astype(F32)]
    fill = cp.shape[1] - (taps + 1) * nb
    pieces = [r[:, WIDE * j : WIDE * j + WIDE] for j in range(nb) for r in rows]
    cp[me] = jnp.concatenate(pieces + [jnp.zeros((fill, WIDE), F32)], 0).astype(BF16)
    loads[0].wait()
    for j in range(nb):
        w1[me, wide * j : wide * j + wide, :] = xwv[:, WIDE * j : WIDE * j + WIDE]
    pl.semaphore_wait(barrier, D - 1 + X - 1 + 1)

    after = lax.rem(me + 1, D)
    halo_copy = pltpu.make_async_remote_copy(
        src_ref=x_hbm.at[pl.ds(tokens - ROWS8, ROWS8)], dst_ref=halo, send_sem=hsem.at[0], recv_sem=hsem.at[1],
        device_id={"a": after // B, "b": lax.rem(after, B)}, device_id_type=MESH,
    )
    first = Gather(sizes, place, 0, w1, sems, cp, (cz, cy, cr))
    second = Gather(sizes, place, 1, w2, sems)
    first.begin()
    halo_copy.start()

    for j in range(nb):
        cols = slice(WIDE * j, WIDE * j + WIDE)
        rate = -jnp.exp(al_ref[:, cols]) * LOG2E
        high = rate.astype(BF16)
        base = j * span + rank
        w2[me, base : base + states, :] = high
        w2[me, base + PACK : base + PACK + states, :] = (rate - high.astype(F32)).astype(BF16)
        two = jnp.concatenate([db_ref[:, cols], sk_ref[:, cols]], 0)
        top = two.astype(BF16).astype(F32)
        w2[me, base + 2 * PACK : base + 3 * PACK, :] = jnp.concatenate(
            [top, two - top, jnp.zeros((PACK - 4, WIDE), F32)], 0
        ).astype(BF16)
    loads[1].wait()
    for j in range(nb):
        w2[me, j * span : j * span + rank, :] = dtv[:, WIDE * j : WIDE * j + WIDE]
    loads[2].wait()
    acc[...] = jnp.zeros_like(acc)
    halo_copy.wait_recv()
    lead = (me > 0).astype(F32)

    def convolve(i):
        s = first.shard(i)
        weight = cp[s].astype(F32)
        for j in range(nb):
            cols = pl.ds(pl.multiple_of(s * shard + WIDE * j, WIDE), WIDE)
            row = lambda n: weight[(taps + 1) * j + n : (taps + 1) * j + n + 1]
            cur = xv[:, cols].astype(F32)
            ext = jnp.concatenate([halo[:, cols].astype(F32) * lead, cur], 0)
            total = row(taps) + row(taps - 1) * cur
            for tap in range(taps - 1):
                low = ROWS8 - taps + 1 + tap
                total = total + row(tap) * ext[low : low + tokens]
            xv[:, cols] = silu(total).astype(BF16)

    def project(i):
        s = first.shard(i)
        total = acc[...]
        for j in range(nb):
            cols = pl.ds(pl.multiple_of(s * shard + WIDE * j, WIDE), WIDE)
            total = total + lax.dot_general(
                xv[:, cols], w1[s, wide * j : wide * j + wide, :], (((1,), (1,)), ((), ())), preferred_element_type=F32
            )
        acc[...] = total

    def step_first(i, _):
        @pl.when(i > 0)
        def _():
            first.relay(i)

        @pl.when(i > 1)
        def _():
            first.relay_plane(i - 1)

        convolve(i)

        @pl.when(i > 2)
        def _():
            first.ready(i - 2)

        @pl.when(i > 1)
        def _():
            project(i - 2)

        return 0

    with jax.named_scope("w1a"):
        lax.fori_loop(0, A, step_first, 0)
    second.begin()
    with jax.named_scope("w1b"):
        lax.fori_loop(A, D, step_first, 0)
    with jax.named_scope("w1c"):
        first.relay_plane(D - 1)
        first.ready(D - 2)
        project(D - 2)
        first.ready(D - 1)
        project(D - 1)

    with jax.named_scope("norm"):
        low = acc[:, :rank]
        nm[...] = (
            low * lax.rsqrt(jnp.mean(low * low, axis=1, keepdims=True) + 1e-06) * gain_ref[...]
        ).astype(BF16)
        bc = acc[:, rank:]
        for n in range(states):
            at = pl.ds(n, tokens, stride=states)
            bx[at, :] = jnp.broadcast_to(bc[:, n : n + 1], (tokens, LANES))
            cx[at, :] = jnp.broadcast_to(bc[:, states + n : states + n + 1], (tokens, LANES))

    tiles = GROUP // LANES
    blocks = GROUP // WIDE
    local_order = groups == D

    def strips(part):
        return [slice(LANES * j, LANES * j + LANES) for j in range(part, part + TILES)]

    def group_at(i):
        return second.shard(i) if local_order else i

    def to_combiner(g):
        return pltpu.make_async_remote_copy(
            src_ref=eb.at[g], dst_ref=rb.at[me], send_sem=es.at[g], recv_sem=er.at[me],
            device_id={"a": g // B, "b": lax.rem(g, B)}, device_id_type=MESH,
        )

    def pass_one(i, _):
        if local_order:
            @pl.when(i + 2 < D)
            def _():
                second.relay(i + 2)

            @pl.when(i + 1 < D)
            def _():
                second.relay_plane(i + 1)

            @pl.when(i > 0)
            def _():
                second.ready(i)

        g = group_at(i)
        sums = []
        for q in range(blocks):
            cb = g * blocks + q
            s, j = cb // nb, lax.rem(cb, nb)
            cols = pl.ds(pl.multiple_of(cb * WIDE, WIDE), WIDE)
            base = pl.multiple_of(j * span, PACK)
            rows = lambda n: pl.ds(pl.multiple_of(base + rank + n * PACK, PACK), PACK)
            misc = w2[s, rows(2), :].astype(F32)
            rt[g, :, WIDE * q : WIDE * q + WIDE] = w2[s, rows(0), :].astype(F32) + w2[s, rows(1), :].astype(F32)
            raw = jnp.dot(nm[...], w2[s, pl.ds(base, rank), :], preferred_element_type=F32)
            raw = raw + (misc[0:1] + misc[2:3])
            small = jnp.exp2(jnp.abs(raw) * -LOG2E)
            step = jnp.maximum(raw, 0.0) + LN2 * jnp.log2(1.0 + small)
            st[:, :, cols] = step.reshape(tokens // ROWS8, ROWS8, WIDE)
            dr[:, :, cols] = (step * xv[:, cols].astype(F32)).reshape(tokens // ROWS8, ROWS8, WIDE)
            total = jnp.sum(step, axis=0, keepdims=True)
            sums += [total[:, :LANES], total[:, LANES:]]
        view = pl.ds(pl.multiple_of(g * GROUP, GROUP), GROUP)
        zero = jnp.zeros((ROWS8, LANES), F32)
        for part in range(0, tiles, TILES):
            h = scan_tokens(
                st.at[:, :, view], dr.at[:, :, view], bx, rt.at[g], (zero,) * (2 * TILES), tokens, strips(part)
            )
            for j in range(TILES):
                n = 16 * (part + j)
                eb[g, n : n + 16, :] = jnp.concatenate([h[j], h[TILES + j]], 0).astype(BF16)
        sums = jnp.concatenate(sums, 0)
        top = sums.astype(BF16).astype(F32)
        eb[g, 16 * tiles : 16 * tiles + 16, :] = jnp.concatenate([top, sums - top], 0).astype(BF16)

        @pl.when(g != me)
        def _():
            to_combiner(g).start()

        @pl.when(g == me)
        def _():
            rb[me] = eb[me]

        return 0

    if local_order:
        second.relay(1)
    else:
        def settle(i, _):
            second.relay(i)
            second.relay_plane(i)
            second.ready(i)
            return 0

        lax.fori_loop(1, D, settle, 0)
    with jax.named_scope("pass1"):
        lax.fori_loop(0, groups, pass_one, 0)

    def to_owner(k):
        return pltpu.make_async_remote_copy(
            src_ref=sb.at[k], dst_ref=h0b.at[me], send_sem=bs.at[k], recv_sem=br.at[me],
            device_id={"a": k // B, "b": lax.rem(k, B)}, device_id_type=MESH,
        )

    def arrival(k):
        return pltpu.make_async_remote_copy(
            src_ref=rb.at[k], dst_ref=rb.at[k], send_sem=es.at[0], recv_sem=er.at[k],
            device_id={"c": c}, device_id_type=MESH,
        )

    with jax.named_scope("combine"):
        @pl.when(me < groups)
        def _():
            def combine(k, start):
                @pl.when(k != me)
                def _():
                    arrival(k).wait_recv()

                now = []
                both = rb[k, 16 * tiles : 16 * tiles + 16, :].astype(F32)
                sums = both[0:8] + both[8:16]
                for j in range(tiles):
                    sb[k, 16 * j : 16 * j + 16, :] = start[j].astype(BF16)
                    decay = jnp.exp2(sums[j : j + 1, :] * rt[me, :, LANES * j : LANES * j + LANES])
                    now.append(decay * start[j] + rb[k, 16 * j : 16 * j + 16, :].astype(F32))

                @pl.when(k != me)
                def _():
                    to_owner(k).start()

                @pl.when(k == me)
                def _():
                    h0b[me] = sb[me]

                return tuple(now)

            lax.fori_loop(0, D, combine, (jnp.zeros((16, LANES), F32),) * tiles)

    loads[3].wait()

    def start_of(g):
        return pltpu.make_async_remote_copy(
            src_ref=h0b.at[g], dst_ref=h0b.at[g], send_sem=bs.at[0], recv_sem=br.at[g],
            device_id={"c": c}, device_id_type=MESH,
        )

    def put(g):
        view = pl.ds(pl.multiple_of(g * GROUP, GROUP), GROUP)
        return pltpu.make_async_copy(gv.at[:, view], out_hbm.at[:, view], osem.at[g])

    def pass_two(i, _):
        g = lax.rem(me + i, groups)

        @pl.when(g != me)
        def _():
            start_of(g).wait_recv()

        view = pl.ds(pl.multiple_of(g * GROUP, GROUP), GROUP)
        xg, gg = xv.at[:, view], gv.at[:, view]
        direct = []
        for q in range(blocks):
            cb = g * blocks + q
            s, j = cb // nb, lax.rem(cb, nb)
            misc = w2[s, pl.ds(pl.multiple_of(j * span + rank + 2 * PACK, PACK), PACK), :].astype(F32)
            both = misc[1:2] + misc[3:4]
            direct += [both[:, LANES * n : LANES * n + LANES] for n in range(WIDE // LANES)]
        for part in range(0, tiles, TILES):
            cols = strips(part)
            first_state = [h0b[g, 16 * j : 16 * j + 16, :].astype(F32) for j in range(part, part + TILES)]
            h = tuple(v[:8] for v in first_state) + tuple(v[8:] for v in first_state)

            def each(i, u, at, now):
                c0, c1 = (cx[pl.ds(at + 8 * k, 8), :] for k in range(2))
                for j in range(TILES):
                    n = PITCH * (STEP * j + u)
                    zb[n : n + 8, :] = c0 * now[0][j] + c1 * now[1][j]
                if u < STEP - 1:
                    return
                where = pl.ds(pl.multiple_of(i * STEP, STEP), STEP)
                for j in range(TILES):
                    halves = []
                    for t in range(0, STEP, 8):
                        o = [zb[pl.ds(PITCH * (STEP * j + t) + q, 8, stride=PITCH), :] for q in range(8)]
                        halves.append(((o[0] + o[1]) + (o[2] + o[3])) + ((o[4] + o[5]) + (o[6] + o[7])))
                    y = jnp.concatenate(halves, 0) + direct[part + j] * xg[where, cols[j]].astype(F32)
                    gg[where, cols[j]] = (y * silu(gg[where, cols[j]].astype(F32))).astype(BF16)

            scan_tokens(st.at[:, :, view], dr.at[:, :, view], bx, rt.at[g], h, tokens, cols, each)
        put(g).start()
        return 0

    with jax.named_scope("pass2"):
        lax.fori_loop(0, groups, pass_two, 0)

    def finish(g, _):
        put(g).wait()

        @pl.when(g != me)
        def _():
            to_combiner(g).wait_send()

        return 0

    with jax.named_scope("finish"):
        lax.fori_loop(0, groups, finish, 0)

        @pl.when(me < groups)
        def _():
            def sent(k, _):
                @pl.when(k != me)
                def _():
                    to_owner(k).wait_send()

                return 0

            lax.fori_loop(0, D, sent, 0)

        halo_copy.wait_send()
        first.drain()
        second.drain()


def local(sizes, conv_input, gate_input, conv_weight, conv_bias, x_weight, dt_gain, dt_weight, dt_bias, a_log, skip):
    A, B, X = sizes
    D = A * B
    tokens, inner = conv_input.shape
    rank, shard = dt_weight.shape
    states = a_log.shape[0]
    nb = shard // WIDE
    groups = inner // GROUP
    small = -(-(conv_weight.shape[0] + 1) * nb // PACK) * PACK
    r1 = padded_rows(x_weight.shape[1] * nb, X)
    r2 = padded_rows((rank + 3 * PACK) * nb, X)
    tiles = GROUP // LANES
    packet = 16 * tiles + 16
    hbm = pl.BlockSpec(memory_space=pl.ANY)
    vmem = pl.BlockSpec(memory_space=pltpu.VMEM)
    dma = pltpu.SemaphoreType.DMA
    return pl.pallas_call(
        functools.partial(mixer_kernel, sizes, states),
        in_specs=[hbm] * 4 + [vmem] * 6,
        out_specs=hbm,
        out_shape=jax.ShapeDtypeStruct((tokens, inner), BF16),
        scratch_shapes=[
            pltpu.VMEM((tokens, inner), BF16),
            pltpu.VMEM((tokens, inner), BF16),
            pltpu.VMEM((x_weight.shape[1], shard), BF16),
            pltpu.VMEM(dt_weight.shape, BF16),
            pltpu.VMEM((ROWS8, inner), BF16),
            pltpu.VMEM((D, small, WIDE), BF16),
            pltpu.VMEM((D, r1, WIDE), BF16),
            pltpu.VMEM((D, r2, WIDE), BF16),
            pltpu.VMEM((tokens, x_weight.shape[1]), F32),
            pltpu.VMEM((tokens, rank), BF16),
            pltpu.VMEM((tokens * states, LANES), F32),
            pltpu.VMEM((tokens * states, LANES), F32),
            pltpu.VMEM((tokens // ROWS8, ROWS8, inner), F32),
            pltpu.VMEM((tokens // ROWS8, ROWS8, inner), F32),
            pltpu.VMEM((groups, states, GROUP), F32),
            pltpu.VMEM((PITCH * STEP * TILES, LANES), F32),
            pltpu.VMEM((groups, packet, LANES), BF16),
            pltpu.VMEM((D, packet, LANES), BF16),
            pltpu.VMEM((D, 16 * tiles, LANES), BF16),
            pltpu.VMEM((groups, 16 * tiles, LANES), BF16),
            dma((4,)), dma((groups,)), dma((2,)), dma((2, A)), dma((B, A)), dma((D,)),
            dma((2, 2, A)), dma((2, B, A)), dma((2, X, D)), dma((2, X, D)),
            dma((2, D)), dma((2, X, D)), dma((2, X, D)),
            dma((groups,)), dma((D,)), dma((D,)), dma((groups,)),
        ],
        compiler_params=pltpu.CompilerParams(
            collective_id=0, has_side_effects=True, vmem_limit_bytes=60 * 1024 * 1024
        ),
        name="mixer",
    )(
        conv_input, gate_input, x_weight.T, dt_weight, conv_weight, conv_bias[None, :], dt_bias[None, :],
        skip[None, :], a_log, dt_gain[None, :],
    )


def solution(mesh):
    seq, batch = mesh.shape["seq"], mesh.shape["batch"]
    cores = 2
    A = math.gcd(seq, batch)
    B, X = seq // A, batch // cores
    grid = Mesh(mesh.devices.reshape(A, B, X, cores), ("a", "b", "x", "c"))
    seqs = ("a", "b")
    rows = P(("x", "c", "a", "b"), None)
    return jax.shard_map(
        functools.partial(local, (A, B, X)),
        mesh=grid,
        in_specs=(
            rows, rows, P(None, seqs), P(seqs), P(seqs, None), P(), P(None, seqs), P(seqs), P(None, seqs), P(seqs),
        ),
        out_specs=rows,
        check_vma=False,
    )
```

time: 123 us -> 102 us (0.83)
  the two profiles are of different devices: /device:TPU:28 before, /device:TPU:20 now
where the time goes in v2:
time: 102 us
  Pallas kernels  97.2 us (95%)
  local copies, waits for them, and re-layouts  4.37 us (4%)
    pallas_call x1, Pallas kernels, local(): pl.pallas_call(functools.partial(mixer_kernel, sizes, states), in_specs=[...  97.2 us
    unnamed x1, local copies, waits for them, and re-layouts  3.1 us

profile of v2, /device:TPU:20, one launch (start us, length us, event | category | flops | bytes accessed | tf_op | source)
XLA Modules:
  0.0 101.5 jit_solution(9235917148356797777)
XLA Ops:
  0.0 1.3 %broadcast_in_dim.12.cb_ref = bf16[1,1024]{1,0:T(2,128)(2,1)} reshape(bf16[1024]{0:T(1024)(128)(2,1)} %param.13) | data formatting | bytes 4096 | tf_op jit(solution)/shard_map/broadcast_in_dim | solution.py:622
  1.3 97.2 %mixer.1 = bf16[128,8192]{1,0:T(8,128)(2,1)} custom-call(bf16[128,8192]{1,0:T(8,128)(2,1)} %x_hbm.1, bf16[128,8192]{1,0:T(8,128)(2,1)} %g_hbm.1, bf16[288,1024]{1,0:T(8,128)(2,1)} %bitcast.4, bf16[256,1024]{1,0:T(8,128)(2,1)} %dtw_hbm.1, bf16[4,1024]{1,0:T(4,128)(2,1)} %cw_ref.1, bf16[1,1024]{1,0:T(2,128)(2,1)} %broadcast_in_dim.12.cb_ref, ...), custom_call_target="tpu_custom_call" | custom-call | tf_op jit(solution)/shard_map/mixer/pallas_call | solution.py:586
  98.4 3.1 %copy.12 = bf16[128,8192]{1,0:T(8,128)(2,1)} copy(bf16[128,8192]{1,0:T(8,128)(2,1)} %mixer.1) | data formatting | bytes 4194304

commit v3 on v2

--- a/solution.py
+++ b/solution.py
@@ -44,27 +44,39 @@
     return jnp.where(i <= 2 * jnp.minimum(a, size - 1 - a), inner, outer)
 
 
+def pieces_of(blocks):
+    return 2 if blocks % 2 == 0 else 1
+
+
 class Gather:
-    def __init__(self, sizes, place, which, buf, sems, small=None, small_sems=None):
+    def __init__(self, sizes, place, which, buf, base, rows, sems, small=None, small_sems=None):
         self.A, self.B, self.X = sizes
         self.a, self.b, self.x, self.c = place
         self.w = which
         self.buf = buf
+        self.base = base
         (self.zs, self.ys, self.xs, self.ds, self.wr, self.xr, self.dr) = sems
         self.small = small
         self.small_sems = small_sems
-        self.half, self.private, self.shared = split_rows(buf.shape[1], self.X)
-
-    def shard(self, i):
+        self.half, self.private, self.shared = split_rows(rows, self.X)
+
+    def turn(self, t):
+        block, r = (t - 1) // self.B, lax.rem(t - 1 + self.B, self.B)
+        r = r + jnp.where(block == self.A - 1, 1, 0)
+        near = jnp.where(r == 0, block + 1, r * self.A + block)
+        return jnp.where(t == 0, 0, near)
+
+    def shard(self, t):
+        i = self.turn(t)
         a = column(self.a, lax.rem(i, self.A), self.A)
         return a * self.B + lax.rem(self.b - i // self.A + self.B, self.B)
 
     def window(self, s, core):
-        start = core * self.half + self.x * self.private
+        start = self.base + core * self.half + self.x * self.private
         return self.buf.at[s, pl.ds(pl.multiple_of(start, PACK), self.private + self.shared)]
 
     def own(self, s, core, plane):
-        start = core * self.half + plane * (self.private + self.shared)
+        start = self.base + core * self.half + plane * (self.private + self.shared)
         return self.buf.at[s, pl.ds(pl.multiple_of(start, PACK), self.private)]
 
     def copy(self, ref, send, recv, **to):
@@ -129,20 +141,22 @@
         for copy in copies:
             copy.wait_send()
 
-    def begin(self):
+    def begin_line(self):
         self.sends(self.a, self.a >= 0, self.a >= 0, self.start)
+
+    def begin_side(self):
         for k in range(1, self.B):
             self.start(self.across(self.a, k))
 
-    def relay(self, i):
-        s = self.shard(i)
+    def relay(self, t):
+        s = self.shard(t)
         p = s // self.B
         if self.small is not None:
             zs, _, wr = self.small_sems
             self.copy(self.small.at[s], zs.at[0, 0], wr.at[s], c=self.c).wait_recv()
         self.copy(self.window(s, self.c), self.zs.at[self.w, 0, 0], self.wr.at[self.w, s], c=self.c).wait_recv()
 
-        @pl.when(i < self.A)
+        @pl.when(lax.rem(s, self.B) == self.b)
         def _():
             self.sends(p, p < self.a, p > self.a, self.start)
             for k in range(1, self.B):
@@ -215,7 +229,7 @@
     sizes, states,
     x_hbm, g_hbm, xw_hbm, dtw_hbm, cw_ref, cb_ref, db_ref, sk_ref, al_ref, gain_ref,
     out_hbm,
-    xv, gv, xwv, dtv, halo, cp, w1, w2, acc, nm, bx, cx, st, dr, rt, zb,
+    xv, gv, xwv, dtv, last, halo_out, halo, cp, w1, w2, acc, nm, bx, cx, st, dr, rt, zb,
     eb, rb, sb, h0b,
     lsem, osem, hsem, cz, cy, cr,
     zs, ys, xs, ds, wr, xr, dr_sem,
@@ -230,6 +244,11 @@
     taps = cw_ref.shape[0]
     groups = inner // GROUP
     span = rank + 3 * PACK
+    cuts = pieces_of(nb)
+    part_blocks = nb // cuts
+    rows1, rows2 = w1.shape[1] // cuts, w2.shape[1] // cuts
+    spot1 = lambda j: (j // part_blocks) * rows1 + (j % part_blocks) * wide
+    spot2 = lambda j: (j // part_blocks) * rows2 + (j % part_blocks) * span
     a, b, x, c = (lax.axis_index(n) for n in ("a", "b", "x", "c"))
     me = a * B + b
     place = (a, b, x, c)
@@ -237,10 +256,10 @@
 
     loads = [
         pltpu.make_async_copy(src, dst, lsem.at[n])
-        for n, (src, dst) in enumerate(((xw_hbm, xwv), (dtw_hbm, dtv), (x_hbm, xv), (g_hbm, gv)))
+        for n, (src, dst) in enumerate(((xw_hbm, xwv), (dtw_hbm, dtv), (x_hbm, xv), (g_hbm, gv), (x_hbm.at[pl.ds(tokens - ROWS8, ROWS8)], last)))
     ]
-    for load in loads:
-        load.start()
+    for n in (4, 0, 1, 2, 3):
+        loads[n].start()
 
     barrier = pltpu.get_barrier_semaphore()
     for r in range(1, D):
@@ -252,30 +271,47 @@
         pl.semaphore_signal(barrier, inc=1, device_id={"x": lax.rem(x + k, X)}, device_id_type=MESH)
     pl.semaphore_signal(barrier, inc=1, device_id={"c": 1 - c}, device_id_type=MESH)
 
-    rows = [cw_ref[...].astype(F32), cb_ref[...].astype(F32)]
+    lanes = cb_ref[...].astype(F32)
+    per = WIDE // LANES
+    bias = lambda j: jnp.concatenate([lanes[n : n + 1] for n in range(per * j, per * j + per)], 1)
+    weight = cw_ref[...].astype(F32)
+    pieces = [r for j in range(nb) for r in (weight[:, WIDE * j : WIDE * j + WIDE], bias(j))]
     fill = cp.shape[1] - (taps + 1) * nb
-    pieces = [r[:, WIDE * j : WIDE * j + WIDE] for j in range(nb) for r in rows]
     cp[me] = jnp.concatenate(pieces + [jnp.zeros((fill, WIDE), F32)], 0).astype(BF16)
+    loads[4].wait()
+    tail = last[...].astype(F32)
+    fill = halo.shape[1] - (taps - 1) * nb
+    for s in range(D):
+        pieces = [
+            tail[ROWS8 - taps + 1 :, n : n + WIDE] for n in range(s * shard, s * shard + shard, WIDE)
+        ]
+        halo_out[s] = jnp.concatenate(pieces + [jnp.zeros((fill, WIDE), F32)], 0).astype(BF16)
     loads[0].wait()
     for j in range(nb):
-        w1[me, wide * j : wide * j + wide, :] = xwv[:, WIDE * j : WIDE * j + WIDE]
-    pl.semaphore_wait(barrier, D - 1 + X - 1 + 1)
+        w1[me, spot1(j) : spot1(j) + wide, :] = xwv[:, WIDE * j : WIDE * j + WIDE]
+    with jax.named_scope("barrier"):
+        pl.semaphore_wait(barrier, D - 1 + X - 1 + 1)
 
     after = lax.rem(me + 1, D)
     halo_copy = pltpu.make_async_remote_copy(
-        src_ref=x_hbm.at[pl.ds(tokens - ROWS8, ROWS8)], dst_ref=halo, send_sem=hsem.at[0], recv_sem=hsem.at[1],
+        src_ref=halo_out, dst_ref=halo, send_sem=hsem.at[0], recv_sem=hsem.at[1],
         device_id={"a": after // B, "b": lax.rem(after, B)}, device_id_type=MESH,
     )
-    first = Gather(sizes, place, 0, w1, sems, cp, (cz, cy, cr))
-    second = Gather(sizes, place, 1, w2, sems)
-    first.begin()
+    first = [
+        Gather(sizes, place, n, w1, n * rows1, rows1, sems, *((cp, (cz, cy, cr)) if n == 0 else ()))
+        for n in range(cuts)
+    ]
+    second = [Gather(sizes, place, cuts + n, w2, n * rows2, rows2, sems) for n in range(cuts)]
     halo_copy.start()
+    for g in first:
+        g.begin_line()
+        g.begin_side()
 
     for j in range(nb):
         cols = slice(WIDE * j, WIDE * j + WIDE)
         rate = -jnp.exp(al_ref[:, cols]) * LOG2E
         high = rate.astype(BF16)
-        base = j * span + rank
+        base = spot2(j) + rank
         w2[me, base : base + states, :] = high
         w2[me, base + PACK : base + PACK + states, :] = (rate - high.astype(F32)).astype(BF16)
         two = jnp.concatenate([db_ref[:, cols], sk_ref[:, cols]], 0)
@@ -285,20 +321,22 @@
         ).astype(BF16)
     loads[1].wait()
     for j in range(nb):
-        w2[me, j * span : j * span + rank, :] = dtv[:, WIDE * j : WIDE * j + WIDE]
+        w2[me, spot2(j) : spot2(j) + rank, :] = dtv[:, WIDE * j : WIDE * j + WIDE]
     loads[2].wait()
     acc[...] = jnp.zeros_like(acc)
-    halo_copy.wait_recv()
     lead = (me > 0).astype(F32)
+    shard_at = first[0].shard
 
     def convolve(i):
-        s = first.shard(i)
+        s = shard_at(i)
         weight = cp[s].astype(F32)
+        before = halo[s].astype(F32) * lead
         for j in range(nb):
             cols = pl.ds(pl.multiple_of(s * shard + WIDE * j, WIDE), WIDE)
             row = lambda n: weight[(taps + 1) * j + n : (taps + 1) * j + n + 1]
             cur = xv[:, cols].astype(F32)
-            ext = jnp.concatenate([halo[:, cols].astype(F32) * lead, cur], 0)
+            head = before[(taps - 1) * j : (taps - 1) * (j + 1)]
+            ext = jnp.concatenate([jnp.zeros((ROWS8 - taps + 1, WIDE), F32), head, cur], 0)
             total = row(taps) + row(taps - 1) * cur
             for tap in range(taps - 1):
                 low = ROWS8 - taps + 1 + tap
@@ -306,46 +344,62 @@
             xv[:, cols] = silu(total).astype(BF16)
 
     def project(i):
-        s = first.shard(i)
+        s = shard_at(i)
+        if not isinstance(i, int) or i > 0:
+            for g in first:
+                g.ready(i)
         total = acc[...]
         for j in range(nb):
             cols = pl.ds(pl.multiple_of(s * shard + WIDE * j, WIDE), WIDE)
             total = total + lax.dot_general(
-                xv[:, cols], w1[s, wide * j : wide * j + wide, :], (((1,), (1,)), ((), ())), preferred_element_type=F32
+                xv[:, cols], w1[s, spot1(j) : spot1(j) + wide, :], (((1,), (1,)), ((), ())),
+                preferred_element_type=F32,
             )
         acc[...] = total
 
-    def step_first(i, _):
-        @pl.when(i > 0)
-        def _():
-            first.relay(i)
-
-        @pl.when(i > 1)
-        def _():
-            first.relay_plane(i - 1)
-
-        convolve(i)
-
-        @pl.when(i > 2)
-        def _():
-            first.ready(i - 2)
-
-        @pl.when(i > 1)
-        def _():
-            project(i - 2)
+    def step_first(t, _):
+        for g in first:
+            g.relay(t)
+
+        @pl.when(t > 2)
+        def _():
+            for g in first:
+                g.relay_plane(t - 2)
+
+        @pl.when(t == 1)
+        def _():
+            halo_copy.wait_recv()
+
+        convolve(t - 1)
+
+        @pl.when(t > 4)
+        def _():
+            project(t - 4)
 
         return 0
 
+    split = (A - 2) * B + 2
     with jax.named_scope("w1a"):
-        lax.fori_loop(0, A, step_first, 0)
-    second.begin()
+        lax.fori_loop(1, split, step_first, 0)
+        for w in second:
+            w.begin_line()
+        lax.fori_loop(split, D, step_first, 0)
+        for w in second:
+            w.begin_side()
     with jax.named_scope("w1b"):
-        lax.fori_loop(A, D, step_first, 0)
-    with jax.named_scope("w1c"):
-        first.relay_plane(D - 1)
-        first.ready(D - 2)
+        convolve(D - 1)
+        for g in first:
+            g.relay_plane(D - 2)
+        project(0)
+        for w in second:
+            w.relay(1)
+        for g in first:
+            g.relay_plane(D - 1)
+        project(D - 4)
+        project(D - 3)
+        for w in second:
+            w.relay(2)
         project(D - 2)
-        first.ready(D - 1)
         project(D - 1)
 
     with jax.named_scope("norm"):
@@ -367,7 +421,7 @@
         return [slice(LANES * j, LANES * j + LANES) for j in range(part, part + TILES)]
 
     def group_at(i):
-        return second.shard(i) if local_order else i
+        return shard_at(i) if local_order else i
 
     def to_combiner(g):
         return pltpu.make_async_remote_copy(
@@ -377,17 +431,20 @@
 
     def pass_one(i, _):
         if local_order:
-            @pl.when(i + 2 < D)
+            @pl.when(i + 3 < D)
             def _():
-                second.relay(i + 2)
+                for w in second:
+                    w.relay(i + 3)
 
             @pl.when(i + 1 < D)
             def _():
-                second.relay_plane(i + 1)
+                for w in second:
+                    w.relay_plane(i + 1)
 
             @pl.when(i > 0)
             def _():
-                second.ready(i)
+                for w in second:
+                    w.ready(i)
 
         g = group_at(i)
         sums = []
@@ -395,7 +452,7 @@
             cb = g * blocks + q
             s, j = cb // nb, lax.rem(cb, nb)
             cols = pl.ds(pl.multiple_of(cb * WIDE, WIDE), WIDE)
-            base = pl.multiple_of(j * span, PACK)
+            base = pl.multiple_of(spot2(j), PACK)
             rows = lambda n: pl.ds(pl.multiple_of(base + rank + n * PACK, PACK), PACK)
             misc = w2[s, rows(2), :].astype(F32)
             rt[g, :, WIDE * q : WIDE * q + WIDE] = w2[s, rows(0), :].astype(F32) + w2[s, rows(1), :].astype(F32)
@@ -430,15 +487,17 @@
 
         return 0
 
-    if local_order:
-        second.relay(1)
-    else:
-        def settle(i, _):
-            second.relay(i)
-            second.relay_plane(i)
-            second.ready(i)
-            return 0
-
+    def settle(i, _):
+        for w in second:
+            @pl.when(i > 2)
+            def _():
+                w.relay(i)
+
+            w.relay_plane(i)
+            w.ready(i)
+        return 0
+
+    if not local_order:
         lax.fori_loop(1, D, settle, 0)
     with jax.named_scope("pass1"):
         lax.fori_loop(0, groups, pass_one, 0)
@@ -508,7 +567,7 @@
         for q in range(blocks):
             cb = g * blocks + q
             s, j = cb // nb, lax.rem(cb, nb)
-            misc = w2[s, pl.ds(pl.multiple_of(j * span + rank + 2 * PACK, PACK), PACK), :].astype(F32)
+            misc = w2[s, pl.ds(pl.multiple_of(spot2(j) + rank + 2 * PACK, PACK), PACK), :].astype(F32)
             both = misc[1:2] + misc[3:4]
             direct += [both[:, LANES * n : LANES * n + LANES] for n in range(WIDE // LANES)]
         for part in range(0, tiles, TILES):
@@ -563,8 +622,8 @@
             lax.fori_loop(0, D, sent, 0)
 
         halo_copy.wait_send()
-        first.drain()
-        second.drain()
+        for w in first + second:
+            w.drain()
 
 
 def local(sizes, conv_input, gate_input, conv_weight, conv_bias, x_weight, dt_gain, dt_weight, dt_bias, a_log, skip):
@@ -576,13 +635,16 @@
     nb = shard // WIDE
     groups = inner // GROUP
     small = -(-(conv_weight.shape[0] + 1) * nb // PACK) * PACK
-    r1 = padded_rows(x_weight.shape[1] * nb, X)
-    r2 = padded_rows((rank + 3 * PACK) * nb, X)
+    edge = -(-(conv_weight.shape[0] - 1) * nb // PACK) * PACK
+    cuts = pieces_of(nb)
+    r1 = cuts * padded_rows(x_weight.shape[1] * nb // cuts, X)
+    r2 = cuts * padded_rows((rank + 3 * PACK) * nb // cuts, X)
     tiles = GROUP // LANES
     packet = 16 * tiles + 16
     hbm = pl.BlockSpec(memory_space=pl.ANY)
     vmem = pl.BlockSpec(memory_space=pltpu.VMEM)
     dma = pltpu.SemaphoreType.DMA
+    all_ = 2 * cuts
     return pl.pallas_call(
         functools.partial(mixer_kernel, sizes, states),
         in_specs=[hbm] * 4 + [vmem] * 6,
@@ -594,6 +656,8 @@
             pltpu.VMEM((x_weight.shape[1], shard), BF16),
             pltpu.VMEM(dt_weight.shape, BF16),
             pltpu.VMEM((ROWS8, inner), BF16),
+            pltpu.VMEM((D, edge, WIDE), BF16),
+            pltpu.VMEM((D, edge, WIDE), BF16),
             pltpu.VMEM((D, small, WIDE), BF16),
             pltpu.VMEM((D, r1, WIDE), BF16),
             pltpu.VMEM((D, r2, WIDE), BF16),
@@ -609,9 +673,9 @@
             pltpu.VMEM((D, packet, LANES), BF16),
             pltpu.VMEM((D, 16 * tiles, LANES), BF16),
             pltpu.VMEM((groups, 16 * tiles, LANES), BF16),
-            dma((4,)), dma((groups,)), dma((2,)), dma((2, A)), dma((B, A)), dma((D,)),
-            dma((2, 2, A)), dma((2, B, A)), dma((2, X, D)), dma((2, X, D)),
-            dma((2, D)), dma((2, X, D)), dma((2, X, D)),
+            dma((5,)), dma((groups,)), dma((2,)), dma((2, A)), dma((B, A)), dma((D,)),
+            dma((all_, 2, A)), dma((all_, B, A)), dma((all_, X, D)), dma((all_, X, D)),
+            dma((all_, D)), dma((all_, X, D)), dma((all_, X, D)),
             dma((groups,)), dma((D,)), dma((D,)), dma((groups,)),
         ],
         compiler_params=pltpu.CompilerParams(
@@ -619,7 +683,7 @@
         ),
         name="mixer",
     )(
-        conv_input, gate_input, x_weight.T, dt_weight, conv_weight, conv_bias[None, :], dt_bias[None, :],
+        conv_input, gate_input, x_weight.T, dt_weight, conv_weight, conv_bias.reshape(-1, LANES), dt_bias[None, :],
         skip[None, :], a_log, dt_gain[None, :],
     )
 

time: 102 us -> 92.1 us (0.903)
  Pallas kernels: 97.2 us -> 88.7 us
  local copies, waits for them, and re-layouts: 4.37 us -> 3.1 us
    pallas_call x1, Pallas kernels: 97.2 us -> 88.7 us  [local(): pl.pallas_call(functools.partial(mixer_kernel, sizes, states), in_specs=[...]
    broadcast_in_dim x1 -> x0, local copies, waits for them, and re-layouts: 1.28 us -> none  [local(): conv_bias[None, :]]
where the time goes in v3:
time: 92.1 us; the launch traced here: 91.8 us
  Pallas kernels  88.7 us (96%)
  local copies, waits for them, and re-layouts  3.1 us (3%)
    pallas_call x1, Pallas kernels, local(): pl.pallas_call(functools.partial(mixer_kernel, sizes, states), in_specs=[...  88.7 us
    unnamed x1, local copies, waits for them, and re-layouts  3.1 us

profile of v3, /device:TPU:20, one launch (start us, length us, event | category | flops | bytes accessed | tf_op | source)
XLA Modules:
  0.0 91.8 jit_solution(14902361972437526734)
XLA Ops:
  0.0 88.7 %mixer.1 = bf16[128,8192]{1,0:T(8,128)(2,1)} custom-call(bf16[128,8192]{1,0:T(8,128)(2,1)} %x_hbm.1, bf16[128,8192]{1,0:T(8,128)(2,1)} %g_hbm.1, bf16[288,1024]{1,0:T(8,128)(2,1)} %bitcast.5, bf16[256,1024]{1,0:T(8,128)(2,1)} %dtw_hbm.1, bf16[4,1024]{1,0:T(4,128)(2,1)} %cw_ref.1, bf16[8,128]{1,0:T(8,128)(2,1)} %bitcast.8, f32[1,1024]{1,0:T(1,128)} %bitcast.6, ...), custom_call_target="tpu_custom_call" | custom-call | tf_op jit(solution)/shard_map/mixer/pallas_call | solution.py:648
  88.7 3.1 %copy.12 = bf16[128,8192]{1,0:T(8,128)(2,1)} copy(bf16[128,8192]{1,0:T(8,128)(2,1)} %mixer.1) | data formatting | bytes 4194304

commit v4 on v3

--- a/solution.py
+++ b/solution.py
@@ -16,9 +16,12 @@
 PACK = 16
 WIDE = 256
 GROUP = 1024
-STEP = 16
+STEP = 32
 TILES = 4
 PITCH = 9
+AHEAD = 9
+CUTS = 2
+SHARE = 0.34
 MESH = pl.DeviceIdType.MESH
 F32 = jnp.float32
 BF16 = jnp.bfloat16
@@ -27,7 +30,7 @@
 def split_rows(rows, planes):
     half = rows // 2
     if planes == 2:
-        private = -(-half // (3 * PACK)) * PACK
+        private = round(half * SHARE / PACK) * PACK
         return half, private, half - 2 * private
     return half, half // planes, 0
 
@@ -45,7 +48,7 @@
 
 
 def pieces_of(blocks):
-    return 2 if blocks % 2 == 0 else 1
+    return math.gcd(blocks, CUTS)
 
 
 class Gather:
@@ -55,6 +58,8 @@
         self.w = which
         self.buf = buf
         self.base = base
+        self.settled = False
+        self.middle = (self.a > 0) & (self.a + 1 < self.A)
         (self.zs, self.ys, self.xs, self.ds, self.wr, self.xr, self.dr) = sems
         self.small = small
         self.small_sems = small_sems
@@ -64,6 +69,9 @@
         block, r = (t - 1) // self.B, lax.rem(t - 1 + self.B, self.B)
         r = r + jnp.where(block == self.A - 1, 1, 0)
         near = jnp.where(r == 0, block + 1, r * self.A + block)
+        if self.B == 2 and self.A > 2:
+            near = jnp.where(self.middle & (t == 2), 2, jnp.where(self.middle & (t == 3), self.A, near))
+            near = jnp.where(self.middle & (t == 4), 3, jnp.where(self.middle & (t == 5), self.A + 1, near))
         return jnp.where(t == 0, 0, near)
 
     def shard(self, t):
@@ -148,6 +156,12 @@
         for k in range(1, self.B):
             self.start(self.across(self.a, k))
 
+    def own_sent(self):
+        self.settled = True
+        self.sends(self.a, self.a >= 0, self.a >= 0, self.sent)
+        for k in range(1, self.B):
+            self.sent(self.across(self.a, k))
+
     def relay(self, t):
         s = self.shard(t)
         p = s // self.B
@@ -179,9 +193,12 @@
 
     def drain(self):
         def line(p, _):
-            self.sends(p, p <= self.a, p >= self.a, self.sent)
-            for k in range(1, self.B):
-                self.sent(self.across(p, k))
+            @pl.when((p != self.a) | (not self.settled))
+            def _():
+                self.sends(p, p <= self.a, p >= self.a, self.sent)
+                for k in range(1, self.B):
+                    self.sent(self.across(p, k))
+
             return 0
 
         lax.fori_loop(0, self.A, line, 0)
@@ -303,7 +320,9 @@
     ]
     second = [Gather(sizes, place, cuts + n, w2, n * rows2, rows2, sems) for n in range(cuts)]
     halo_copy.start()
-    for g in first:
+    for n, g in enumerate(first):
+        if n >= AHEAD:
+            first[n - AHEAD].own_sent()
         g.begin_line()
         g.begin_side()
 
@@ -361,10 +380,10 @@
         for g in first:
             g.relay(t)
 
-        @pl.when(t > 2)
+        @pl.when(t > 3)
         def _():
             for g in first:
-                g.relay_plane(t - 2)
+                g.relay_plane(t - 3)
 
         @pl.when(t == 1)
         def _():
@@ -372,9 +391,9 @@
 
         convolve(t - 1)
 
-        @pl.when(t > 4)
-        def _():
-            project(t - 4)
+        @pl.when(t > 5)
+        def _():
+            project(t - 5)
 
         return 0
 
@@ -386,21 +405,27 @@
         lax.fori_loop(split, D, step_first, 0)
         for w in second:
             w.begin_side()
+    middle = second[0].middle
+
+    def second_relay(t, when):
+        @pl.when(when)
+        def _():
+            for w in second:
+                w.relay(t)
+
     with jax.named_scope("w1b"):
         convolve(D - 1)
-        for g in first:
-            g.relay_plane(D - 2)
+        for t in (D - 3, D - 2):
+            for g in first:
+                g.relay_plane(t)
         project(0)
         for w in second:
             w.relay(1)
+        second_relay(2, middle)
         for g in first:
             g.relay_plane(D - 1)
-        project(D - 4)
-        project(D - 3)
-        for w in second:
-            w.relay(2)
-        project(D - 2)
-        project(D - 1)
+        for t in range(D - 5, D):
+            project(t)
 
     with jax.named_scope("norm"):
         low = acc[:, :rank]
@@ -412,6 +437,9 @@
             at = pl.ds(n, tokens, stride=states)
             bx[at, :] = jnp.broadcast_to(bc[:, n : n + 1], (tokens, LANES))
             cx[at, :] = jnp.broadcast_to(bc[:, states + n : states + n + 1], (tokens, LANES))
+        second_relay(2, jnp.logical_not(middle))
+        for w in second:
+            w.relay_plane(1)
 
     tiles = GROUP // LANES
     blocks = GROUP // WIDE
@@ -435,11 +463,6 @@
             def _():
                 for w in second:
                     w.relay(i + 3)
-
-            @pl.when(i + 1 < D)
-            def _():
-                for w in second:
-                    w.relay_plane(i + 1)
 
             @pl.when(i > 0)
             def _():
@@ -470,6 +493,13 @@
             h = scan_tokens(
                 st.at[:, :, view], dr.at[:, :, view], bx, rt.at[g], (zero,) * (2 * TILES), tokens, strips(part)
             )
+            if local_order and part == 0:
+                @pl.when(i + 2 < D)
+                def _():
+                    with jax.named_scope("pl"):
+                        for w in second:
+                            w.relay_plane(i + 2)
+
             for j in range(TILES):
                 n = 16 * (part + j)
                 eb[g, n : n + 16, :] = jnp.concatenate([h[j], h[TILES + j]], 0).astype(BF16)
@@ -493,7 +523,10 @@
             def _():
                 w.relay(i)
 
-            w.relay_plane(i)
+            @pl.when(i > 1)
+            def _():
+                w.relay_plane(i)
+
             w.ready(i)
         return 0
 

time: 92.1 us -> 87.5 us (0.950)
  Pallas kernels: 88.7 us -> 84.2 us
    pallas_call x1, Pallas kernels: 88.7 us -> 84.2 us  [local(): pl.pallas_call(functools.partial(mixer_kernel, sizes, states), in_specs=[...]
where the time goes in v4:
time: 87.5 us; the launch traced here: 87.3 us
  Pallas kernels  84.2 us (96%)
  local copies, waits for them, and re-layouts  3.1 us (4%)
    pallas_call x1, Pallas kernels, local(): pl.pallas_call(functools.partial(mixer_kernel, sizes, states), in_specs=[...  84.2 us
    unnamed x1, local copies, waits for them, and re-layouts  3.1 us

profile of v4, /device:TPU:20, one launch (start us, length us, event | category | flops | bytes accessed | tf_op | source)
XLA Modules:
  0.0 87.3 jit_solution(6674879270731577064)
XLA Ops:
  0.0 84.2 %mixer.1 = bf16[128,8192]{1,0:T(8,128)(2,1)} custom-call(bf16[128,8192]{1,0:T(8,128)(2,1)} %x_hbm.1, bf16[128,8192]{1,0:T(8,128)(2,1)} %g_hbm.1, bf16[288,1024]{1,0:T(8,128)(2,1)} %bitcast.5, bf16[256,1024]{1,0:T(8,128)(2,1)} %dtw_hbm.1, bf16[4,1024]{1,0:T(4,128)(2,1)} %cw_ref.1, bf16[8,128]{1,0:T(8,128)(2,1)} %bitcast.8, f32[1,1024]{1,0:T(1,128)} %bitcast.6, ...), custom_call_target="tpu_custom_call" | custom-call | tf_op jit(solution)/shard_map/mixer/pallas_call | solution.py:681
  84.2 3.1 %copy.12 = bf16[128,8192]{1,0:T(8,128)(2,1)} copy(bf16[128,8192]{1,0:T(8,128)(2,1)} %mixer.1) | data formatting | bytes 4194304

commit v5 on v4

--- a/solution.py
+++ b/solution.py
@@ -22,6 +22,9 @@
 AHEAD = 9
 CUTS = 2
 SHARE = 0.34
+PARTS = 4
+VMEM_MAIN = 48 * 1024 * 1024
+VMEM_COPY = 4 * 1024 * 1024
 MESH = pl.DeviceIdType.MESH
 F32 = jnp.float32
 BF16 = jnp.bfloat16
@@ -245,10 +248,10 @@
 def mixer_kernel(
     sizes, states,
     x_hbm, g_hbm, xw_hbm, dtw_hbm, cw_ref, cb_ref, db_ref, sk_ref, al_ref, gain_ref,
-    out_hbm,
-    xv, gv, xwv, dtv, last, halo_out, halo, cp, w1, w2, acc, nm, bx, cx, st, dr, rt, zb,
+    gv,
+    xv, xwv, dtv, last, halo_out, halo, cp, w1, w2, acc, nm, bx, cx, st, dr, rt, zb,
     eb, rb, sb, h0b,
-    lsem, osem, hsem, cz, cy, cr,
+    lsem, hsem, cz, cy, cr,
     zs, ys, xs, ds, wr, xr, dr_sem,
     es, er, bs, br,
 ):
@@ -547,6 +550,10 @@
             device_id={"c": c}, device_id_type=MESH,
         )
 
+    with jax.named_scope("drain"):
+        for w in first + second:
+            w.drain()
+
     with jax.named_scope("combine"):
         @pl.when(me < groups)
         def _():
@@ -582,10 +589,6 @@
             src_ref=h0b.at[g], dst_ref=h0b.at[g], send_sem=bs.at[0], recv_sem=br.at[g],
             device_id={"c": c}, device_id_type=MESH,
         )
-
-    def put(g):
-        view = pl.ds(pl.multiple_of(g * GROUP, GROUP), GROUP)
-        return pltpu.make_async_copy(gv.at[:, view], out_hbm.at[:, view], osem.at[g])
 
     def pass_two(i, _):
         g = lax.rem(me + i, groups)
@@ -625,14 +628,12 @@
                     gg[where, cols[j]] = (y * silu(gg[where, cols[j]].astype(F32))).astype(BF16)
 
             scan_tokens(st.at[:, :, view], dr.at[:, :, view], bx, rt.at[g], h, tokens, cols, each)
-        put(g).start()
         return 0
 
     with jax.named_scope("pass2"):
         lax.fori_loop(0, groups, pass_two, 0)
 
     def finish(g, _):
-        put(g).wait()
 
         @pl.when(g != me)
         def _():
@@ -655,8 +656,18 @@
             lax.fori_loop(0, D, sent, 0)
 
         halo_copy.wait_send()
-        for w in first + second:
-            w.drain()
+
+
+def write_kernel(y_ref, out_hbm, sem):
+    rows = y_ref.shape[0] // PARTS
+    copies = [
+        pltpu.make_async_copy(y_ref.at[pl.ds(n * rows, rows)], out_hbm.at[pl.ds(n * rows, rows)], sem.at[n])
+        for n in range(PARTS)
+    ]
+    for copy in copies:
+        copy.start()
+    for copy in copies:
+        copy.wait()
 
 
 def local(sizes, conv_input, gate_input, conv_weight, conv_bias, x_weight, dt_gain, dt_weight, dt_bias, a_log, skip):
@@ -674,17 +685,16 @@
     r2 = cuts * padded_rows((rank + 3 * PACK) * nb // cuts, X)
     tiles = GROUP // LANES
     packet = 16 * tiles + 16
-    hbm = pl.BlockSpec(memory_space=pl.ANY)
+    hbm = pl.BlockSpec(memory_space=pltpu.HBM)
     vmem = pl.BlockSpec(memory_space=pltpu.VMEM)
     dma = pltpu.SemaphoreType.DMA
     all_ = 2 * cuts
-    return pl.pallas_call(
+    mixed = pl.pallas_call(
         functools.partial(mixer_kernel, sizes, states),
         in_specs=[hbm] * 4 + [vmem] * 6,
-        out_specs=hbm,
+        out_specs=vmem,
         out_shape=jax.ShapeDtypeStruct((tokens, inner), BF16),
         scratch_shapes=[
-            pltpu.VMEM((tokens, inner), BF16),
             pltpu.VMEM((tokens, inner), BF16),
             pltpu.VMEM((x_weight.shape[1], shard), BF16),
             pltpu.VMEM(dt_weight.shape, BF16),
@@ -706,19 +716,33 @@
             pltpu.VMEM((D, packet, LANES), BF16),
             pltpu.VMEM((D, 16 * tiles, LANES), BF16),
             pltpu.VMEM((groups, 16 * tiles, LANES), BF16),
-            dma((5,)), dma((groups,)), dma((2,)), dma((2, A)), dma((B, A)), dma((D,)),
+            dma((5,)), dma((2,)), dma((2, A)), dma((B, A)), dma((D,)),
             dma((all_, 2, A)), dma((all_, B, A)), dma((all_, X, D)), dma((all_, X, D)),
             dma((all_, D)), dma((all_, X, D)), dma((all_, X, D)),
             dma((groups,)), dma((D,)), dma((D,)), dma((groups,)),
         ],
         compiler_params=pltpu.CompilerParams(
-            collective_id=0, has_side_effects=True, vmem_limit_bytes=60 * 1024 * 1024
+            collective_id=0, has_side_effects=True, vmem_limit_bytes=VMEM_MAIN
         ),
         name="mixer",
     )(
-        conv_input, gate_input, x_weight.T, dt_weight, conv_weight, conv_bias.reshape(-1, LANES), dt_bias[None, :],
-        skip[None, :], a_log, dt_gain[None, :],
+        *(
+            pltpu.with_memory_space_constraint(v, pltpu.HBM)
+            for v in (
+                conv_input, gate_input, x_weight.T, dt_weight, conv_weight, conv_bias.reshape(-1, LANES),
+                dt_bias[None, :], skip[None, :], a_log, dt_gain[None, :],
+            )
+        )
     )
+    return pl.pallas_call(
+        write_kernel,
+        in_specs=[vmem],
+        out_specs=hbm,
+        out_shape=jax.ShapeDtypeStruct((tokens, inner), BF16),
+        scratch_shapes=[dma((PARTS,))],
+        compiler_params=pltpu.CompilerParams(vmem_limit_bytes=VMEM_COPY),
+        name="write",
+    )(mixed)
 
 
 def solution(mesh):

time: 87.5 us -> 83.8 us (0.958)
  local copies, waits for them, and re-layouts: 3.1 us -> 0 us
    unnamed x1 -> x0, local copies, waits for them, and re-layouts: 3.1 us -> none
    pallas_call x1, Pallas kernels: 84.2 us -> 82.3 us  [local(): pl.pallas_call(functools.partial(mixer_kernel, sizes, states), in_specs=[...]
    pallas_call x0 -> x1, Pallas kernels: none -> 1.35 us  [local(): pl.pallas_call(write_kernel, in_specs=[vmem], out_specs=hbm, out_shape=ja...]
where the time goes in v5:
time: 83.8 us; the launch traced here: 83.6 us
  Pallas kernels  83.6 us (100%)
    pallas_call x1, Pallas kernels, local(): pl.pallas_call(functools.partial(mixer_kernel, sizes, states), in_specs=[...  82.3 us

profile of v5, /device:TPU:20, one launch (start us, length us, event | category | flops | bytes accessed | tf_op | source)
XLA Modules:
  0.0 83.6 jit_solution(8062941247699778265)
XLA Ops:
  0.0 82.3 %mixer.1.y_ref = bf16[128,8192]{1,0:T(8,128)(2,1)S(1)} custom-call(bf16[128,8192]{1,0:T(8,128)(2,1)} %x_hbm.1, bf16[128,8192]{1,0:T(8,128)(2,1)} %g_hbm.1, bf16[288,1024]{1,0:T(8,128)(2,1)} %bitcast.5, bf16[256,1024]{1,0:T(8,128)(2,1)} %dtw_hbm.1, bf16[4,1024]{1,0:T(4,128)(2,1)} %cw_ref.1, bf16[8,128]{1,0:T(8,128)(2,1)} %bitcast.8, f32[1,1024]{1,0:T(1,128)} %bitcast.6, ...), custom_call_target="tpu_custom_call" | custom-call | tf_op jit(solution)/shard_map/mixer/pallas_call | solution.py:692
  82.3 1.3 %write.1 = bf16[128,8192]{1,0:T(8,128)(2,1)} custom-call(bf16[128,8192]{1,0:T(8,128)(2,1)S(1)} %mixer.1.y_ref), custom_call_target="tpu_custom_call" | custom-call | tf_op jit(solution)/shard_map/write/pallas_call | solution.py:737

commit v6 on v5

--- a/solution.py
+++ b/solution.py
@@ -16,7 +16,7 @@
 PACK = 16
 WIDE = 256
 GROUP = 1024
-STEP = 32
+STEP = 64
 TILES = 4
 PITCH = 9
 AHEAD = 9
@@ -247,11 +247,12 @@
 
 def mixer_kernel(
     sizes, states,
-    x_hbm, g_hbm, xw_hbm, dtw_hbm, cw_ref, cb_ref, db_ref, sk_ref, al_ref, gain_ref,
+    x_hbm, g_hbm, xw_hbm, dtw_hbm, cw_hbm, cb_hbm, db_hbm, sk_hbm, al_hbm, gain_hbm,
     gv,
     xv, xwv, dtv, last, halo_out, halo, cp, w1, w2, acc, nm, bx, cx, st, dr, rt, zb,
     eb, rb, sb, h0b,
-    lsem, hsem, cz, cy, cr,
+    cw_ref, cb_ref, db_ref, sk_ref, al_ref, gain_ref,
+    lsem, ssem, hsem, cz, cy, cr,
     zs, ys, xs, ds, wr, xr, dr_sem,
     es, er, bs, br,
 ):
@@ -274,13 +275,6 @@
     place = (a, b, x, c)
     sems = (zs, ys, xs, ds, wr, xr, dr_sem)
 
-    loads = [
-        pltpu.make_async_copy(src, dst, lsem.at[n])
-        for n, (src, dst) in enumerate(((xw_hbm, xwv), (dtw_hbm, dtv), (x_hbm, xv), (g_hbm, gv), (x_hbm.at[pl.ds(tokens - ROWS8, ROWS8)], last)))
-    ]
-    for n in (4, 0, 1, 2, 3):
-        loads[n].start()
-
     barrier = pltpu.get_barrier_semaphore()
     for r in range(1, D):
         other = lax.rem(me + r, D)
@@ -291,6 +285,25 @@
         pl.semaphore_signal(barrier, inc=1, device_id={"x": lax.rem(x + k, X)}, device_id_type=MESH)
     pl.semaphore_signal(barrier, inc=1, device_id={"c": 1 - c}, device_id_type=MESH)
 
+    loads = [
+        pltpu.make_async_copy(src, dst, lsem.at[n])
+        for n, (src, dst) in enumerate(((xw_hbm, xwv), (dtw_hbm, dtv), (x_hbm, xv), (g_hbm, gv), (x_hbm.at[pl.ds(tokens - ROWS8, ROWS8)], last)))
+    ]
+    for n in (4, 0, 1, 2, 3):
+        loads[n].start()
+
+    smalls = [
+        pltpu.make_async_copy(src, dst, ssem.at[n])
+        for n, (src, dst) in enumerate((
+            (cw_hbm, cw_ref), (cb_hbm, cb_ref), (db_hbm, db_ref), (sk_hbm, sk_ref), (al_hbm, al_ref),
+            (gain_hbm, gain_ref),
+        ))
+    ]
+    for load in smalls:
+        load.start()
+
+    for load in smalls[:2]:
+        load.wait()
     lanes = cb_ref[...].astype(F32)
     per = WIDE // LANES
     bias = lambda j: jnp.concatenate([lanes[n : n + 1] for n in range(per * j, per * j + per)], 1)
@@ -329,6 +342,8 @@
         g.begin_line()
         g.begin_side()
 
+    for load in smalls[2:]:
+        load.wait()
     for j in range(nb):
         cols = slice(WIDE * j, WIDE * j + WIDE)
         rate = -jnp.exp(al_ref[:, cols]) * LOG2E
@@ -689,9 +704,12 @@
     vmem = pl.BlockSpec(memory_space=pltpu.VMEM)
     dma = pltpu.SemaphoreType.DMA
     all_ = 2 * cuts
+    small_inputs = (
+        conv_weight, conv_bias.reshape(-1, LANES), dt_bias[None, :], skip[None, :], a_log, dt_gain[None, :],
+    )
     mixed = pl.pallas_call(
         functools.partial(mixer_kernel, sizes, states),
-        in_specs=[hbm] * 4 + [vmem] * 6,
+        in_specs=[hbm] * 10,
         out_specs=vmem,
         out_shape=jax.ShapeDtypeStruct((tokens, inner), BF16),
         scratch_shapes=[
@@ -716,7 +734,8 @@
             pltpu.VMEM((D, packet, LANES), BF16),
             pltpu.VMEM((D, 16 * tiles, LANES), BF16),
             pltpu.VMEM((groups, 16 * tiles, LANES), BF16),
-            dma((5,)), dma((2,)), dma((2, A)), dma((B, A)), dma((D,)),
+            *(pltpu.VMEM(v.shape, v.dtype) for v in small_inputs),
+            dma((5,)), dma((len(small_inputs),)), dma((2,)), dma((2, A)), dma((B, A)), dma((D,)),
             dma((all_, 2, A)), dma((all_, B, A)), dma((all_, X, D)), dma((all_, X, D)),
             dma((all_, D)), dma((all_, X, D)), dma((all_, X, D)),
             dma((groups,)), dma((D,)), dma((D,)), dma((groups,)),
@@ -729,8 +748,7 @@
         *(
             pltpu.with_memory_space_constraint(v, pltpu.HBM)
             for v in (
-                conv_input, gate_input, x_weight.T, dt_weight, conv_weight, conv_bias.reshape(-1, LANES),
-                dt_bias[None, :], skip[None, :], a_log, dt_gain[None, :],
+                conv_input, gate_input, x_weight.T, dt_weight, *small_inputs
             )
         )
     )

time: 83.8 us -> 82.5 us (0.984)
  Pallas kernels: 83.6 us -> 82.3 us
    pallas_call x1, Pallas kernels: 82.3 us -> 80.9 us  [local(): pl.pallas_call(functools.partial(mixer_kernel, sizes, states), in_specs=[...]
where the time goes in v6:
time: 82.5 us; the launch traced here: 82.3 us
  Pallas kernels  82.3 us (100%)
    pallas_call x1, Pallas kernels, local(): pl.pallas_call(functools.partial(mixer_kernel, sizes, states), in_specs=[...  80.9 us

profile of v6, /device:TPU:20, one launch (start us, length us, event | category | flops | bytes accessed | tf_op | source)
XLA Modules:
  0.0 82.3 jit_solution(12169895271856585805)
XLA Ops:
  0.0 80.9 %mixer.1.y_ref = bf16[128,8192]{1,0:T(8,128)(2,1)S(1)} custom-call(bf16[128,8192]{1,0:T(8,128)(2,1)} %x_hbm.1, bf16[128,8192]{1,0:T(8,128)(2,1)} %g_hbm.1, bf16[288,1024]{1,0:T(8,128)(2,1)} %bitcast.5, bf16[256,1024]{1,0:T(8,128)(2,1)} %dtw_hbm.1, bf16[4,1024]{1,0:T(4,128)(2,1)} %cw_hbm.1, bf16[8,128]{1,0:T(8,128)(2,1)} %bitcast.8, f32[1,1024]{1,0:T(1,128)} %bitcast.6, ...), custom_call_target="tpu_custom_call" | custom-call | tf_op jit(solution)/shard_map/mixer/pallas_call | solution.py:710
  80.9 1.3 %write.1 = bf16[128,8192]{1,0:T(8,128)(2,1)} custom-call(bf16[128,8192]{1,0:T(8,128)(2,1)S(1)} %mixer.1.y_ref), custom_call_target="tpu_custom_call" | custom-call | tf_op jit(solution)/shard_map/write/pallas_call | solution.py:755
